TPU v7x, 128 devices: a whole 4x4x4 slice. The times are simulated.
128 devices in a mesh: rep: 4 (over y_hi, core), dp: 32 (over y_lo, z, x).
Axes of the slice: x: 4, y: 4 (y_hi: 2, y_lo: 2; y = y_hi * 2 + y_lo), z: 4, core: 2. Of those that a mesh axis runs over, the one named last changes fastest.
Arguments:
- query_states: bfloat16 [1024, 32, 768], P(('rep', 'dp')), may hold values from -12 to 12
- passage_states: bfloat16 [512, 180, 768], P(('rep', 'dp')), may hold values from -12 to 12
- query_lengths: int32 [1024], P(('rep', 'dp')), may hold values from 8 to 32, as said below
- passage_lengths: int32 [512], P(('rep', 'dp')), may hold values from 45 to 180, as said below
- passage_ids: int32 [512, 180], P(('rep', 'dp')), may hold values from 2 to 30521, as said below
- positives: int32 [1024], P(('rep', 'dp')), may hold values from 0 to 127, as said below
- up_weight: bfloat16 [768, 3072], replicated, may hold values from -0.21875 to 0.21875
- up_bias: float32 [3072], replicated, may hold values from -3 to 3
- down_weight: bfloat16 [3072, 768], replicated, may hold values from -0.109375 to 0.109375
- down_bias: float32 [768], replicated, may hold values from -3 to 3
- norm_gain: float32 [768], replicated, may hold values from 0.5 to 1.5
- norm_bias: float32 [768], replicated, may hold values from -2 to 2
- proj_weight: bfloat16 [768, 128], replicated, may hold values from -0.21875 to 0.21875
Outputs:
- mean_loss: float32 [], replicated
- passage_grad: float32 [512, 180, 128], P(('rep', 'dp'))
- proj_grad: float32 [768, 128], replicated
Inputs may be any that keep to these rules, and one draw needn't show every extreme that they name: `query_lengths`: every device holds a query with all 32 slots real. `passage_lengths`: every device holds a passage with all 180 slots real. `passage_ids`: slots 0 and 1 of every passage hold ids 101 and 2; ids 999 to 1066 are punctuation. `positives`: index of the positive passage among the 128 passages of the query's replica group, in the order of the devices.
All inputs are finite; a program needn't handle non-finite values.
Results may differ from a plain program's by a relative error of at most 0.0055.
Values may be sent and summed in bfloat16 or wider, within the bound.
A program may use at most 128 MiB of HBM per device.

v0:
```python
import math

import jax
import jax.numpy as jnp
from jax import lax
from jax.sharding import PartitionSpec as P

temper = 0.05
eps_norm = 1e-06
punct_low = 999
punct_high = 1067


def in_one_piece(arrays, axis, dim, along):
    widths = [math.prod(a.shape[along:]) for a in arrays]
    both = jnp.concatenate(
        [a.reshape(*a.shape[:along], w) for a, w in zip(arrays, widths)], axis=along
    )
    out = lax.all_gather(both, axis, axis=dim, tiled=True)
    blocks = jnp.split(out, [sum(widths[:k]) for k in range(1, len(widths))], axis=along)
    return tuple((b.reshape(*out.shape[:along], *a.shape[along:]) for a, b in zip(arrays, blocks)))


def in_blocks(array, dim, peers):
    before, after = (array.shape[:dim], array.shape[dim + 1 :])
    return jnp.moveaxis(array.reshape(*before, peers, -1, *after), dim, 0)


def summed_on_arrival(array, axis, dim):
    blocks = in_blocks(array, dim, lax.axis_size(axis))
    arrived = lax.all_to_all(blocks, axis, split_axis=0, concat_axis=0, tiled=True)
    return arrived.astype(jnp.float32).sum(axis=0)


def encode_rows(
    token_rows, up_weight, up_bias, down_weight, down_bias, norm_gain, norm_bias, proj_weight
):
    upward = jnp.dot(token_rows, up_weight, preferred_element_type=jnp.float32) + up_bias
    activated = jax.nn.gelu(upward, approximate=False).astype(jnp.bfloat16)
    residual = (
        token_rows.astype(jnp.float32)
        + jnp.dot(activated, down_weight, preferred_element_type=jnp.float32)
        + down_bias
    )
    average = jnp.mean(residual, -1, keepdims=True)
    centered = residual - average
    variance = jnp.mean(centered * centered, -1, keepdims=True)
    hidden = (centered * lax.rsqrt(variance + eps_norm) * norm_gain + norm_bias).astype(
        jnp.bfloat16
    )
    projected = jnp.dot(hidden, proj_weight, preferred_element_type=jnp.float32)
    inverse = lax.rsqrt(jnp.sum(projected * projected, -1, keepdims=True) + eps_norm)
    return (hidden, projected * inverse, inverse)


def token_scores(query_flat, query_keep, block_emb, block_keep, query_count):
    item_count, pass_len, embed_dim = block_emb.shape
    flat_block = block_emb.reshape(item_count * pass_len, embed_dim)
    similar = lax.dot_general(
        query_flat, flat_block, (((1,), (1,)), ((), ())), preferred_element_type=jnp.float32
    )
    weights = (
        jnp.exp(similar / temper).reshape(-1, item_count, pass_len)
        * block_keep.astype(jnp.float32)[None]
    )
    totals = jnp.sum(weights, -1)
    soft_max = temper * jnp.log(totals) * query_keep[:, None]
    scores = jnp.sum(soft_max.reshape(query_count, -1, item_count), 1)
    return (scores, weights, totals)


def token_grads(query_flat, query_keep, block_emb, weights, totals, dscore, query_count):
    item_count, pass_len, embed_dim = block_emb.shape
    factor = (dscore[:, None, :] * query_keep.reshape(query_count, -1)[:, :, None]).reshape(
        -1, item_count
    ) / totals
    sim_grad = (
        (weights * factor[:, :, None]).reshape(-1, item_count * pass_len).astype(jnp.bfloat16)
    )
    flat_block = block_emb.reshape(item_count * pass_len, embed_dim)
    passage_term = lax.dot_general(
        sim_grad, query_flat, (((0,), (0,)), ((), ())), preferred_element_type=jnp.float32
    )
    query_term = jnp.dot(sim_grad, flat_block, preferred_element_type=jnp.float32)
    return (passage_term.reshape(item_count, pass_len, embed_dim), query_term)


def cross_entropy(scores, positives):
    log_total = jnp.log(jnp.sum(jnp.exp(scores), 1))
    onehot = (jnp.arange(scores.shape[1], dtype=jnp.int32)[None, :] == positives[:, None]).astype(
        jnp.float32
    )
    loss_sum = jnp.sum(log_total - jnp.sum(scores * onehot, 1))
    dscore = jnp.exp(scores - log_total[:, None]) - onehot
    return (loss_sum, dscore)


def norm_backward(gradient, normed, inverse):
    return (inverse * (gradient - normed * jnp.sum(normed * gradient, -1, keepdims=True))).astype(
        jnp.bfloat16
    )


def per_device(
    query_states,
    passage_states,
    query_lengths,
    passage_lengths,
    passage_ids,
    positives,
    up_weight,
    up_bias,
    down_weight,
    down_bias,
    norm_gain,
    norm_bias,
    proj_weight,
):
    query_count, query_len, model_width = query_states.shape
    pass_count, pass_len, _ = passage_states.shape
    embed_dim = proj_weight.shape[1]
    token_rows = jnp.concatenate(
        [query_states.reshape(-1, model_width), passage_states.reshape(-1, model_width)], 0
    )
    hidden, normed, inverse = encode_rows(
        token_rows, up_weight, up_bias, down_weight, down_bias, norm_gain, norm_bias, proj_weight
    )
    boundary = query_count * query_len
    query_emb = normed[:boundary].astype(jnp.bfloat16)
    pass_emb = normed[boundary:].astype(jnp.bfloat16).reshape(pass_count, pass_len, embed_dim)
    query_keep = (
        (jnp.arange(query_len, dtype=jnp.int32)[None, :] < query_lengths[:, None])
        .astype(jnp.float32)
        .reshape(-1)
    )
    is_punct = (passage_ids >= punct_low) & (passage_ids < punct_high)
    pass_keep = (
        (jnp.arange(pass_len, dtype=jnp.int32)[None, :] < passage_lengths[:, None])
        & jnp.logical_not(is_punct)
    ).astype(jnp.bfloat16)
    groups = lax.axis_size("dp")
    query_shaped = query_emb.reshape(query_count, query_len, embed_dim)
    keep_shaped = query_keep.astype(jnp.bfloat16).reshape(query_count, query_len)
    gathered, gathered_keep = in_one_piece((query_shaped, keep_shaped), "dp", 0, 2)
    group_query = query_count * groups
    block_query = math.gcd(group_query, 16)
    block_count = group_query // block_query
    query_blocks = gathered.reshape(block_count, block_query * query_len, embed_dim)
    keep_blocks = gathered_keep.astype(jnp.float32).reshape(block_count, block_query * query_len)

    def forward(paired):
        scores, _, _ = token_scores(paired[0], paired[1], pass_emb, pass_keep, block_query)
        return scores

    scores = lax.map(forward, (query_blocks, keep_blocks)).reshape(group_query, pass_count)
    owned_rows = lax.all_to_all(scores, "dp", split_axis=0, concat_axis=1, tiled=True)
    loss_sum, dscore = cross_entropy(owned_rows, positives)
    returned = lax.all_to_all(dscore, "dp", split_axis=1, concat_axis=0, tiled=True)
    grad_blocks = returned.reshape(block_count, block_query, pass_count)

    def backward(pass_grad, triple):
        block_emb, block_keep, block_grad = triple
        _, weights, totals = token_scores(block_emb, block_keep, pass_emb, pass_keep, block_query)
        passage_term, query_term = token_grads(
            block_emb, block_keep, pass_emb, weights, totals, block_grad, block_query
        )
        return (pass_grad + passage_term, query_term)

    start_grad = jnp.zeros((pass_count, pass_len, embed_dim), jnp.float32)
    passage_grad, query_terms = lax.scan(
        backward, start_grad, (query_blocks, keep_blocks, grad_blocks)
    )
    query_grad = summed_on_arrival(
        query_terms.reshape(group_query, query_len, embed_dim).astype(jnp.bfloat16), "dp", 0
    )
    query_grad = query_grad.reshape(query_count * query_len, embed_dim)
    query_back = norm_backward(query_grad, normed[:boundary], inverse[:boundary])
    pass_back = norm_backward(
        passage_grad.reshape(-1, embed_dim), normed[boundary:], inverse[boundary:]
    )
    all_back = jnp.concatenate([query_back, pass_back], 0)
    local_sum = lax.dot_general(
        hidden, all_back, (((0,), (0,)), ((), ())), preferred_element_type=jnp.float32
    )
    proj_total, loss_total = lax.psum((local_sum, loss_sum), ("rep", "dp"))
    mean_loss = loss_total / (query_count * lax.axis_size("rep") * groups)
    return (mean_loss, passage_grad, proj_total)


def solution(mesh):
    in_specs = (
        P(("rep", "dp"), None, None),
        P(("rep", "dp"), None, None),
        P(("rep", "dp")),
        P(("rep", "dp")),
        P(("rep", "dp"), None),
        P(("rep", "dp")),
        P(),
        P(),
        P(),
        P(),
        P(),
        P(),
        P(),
    )
    out_specs = (P(), P(("rep", "dp"), None, None), P())
    return jax.shard_map(
        per_device, mesh=mesh, in_specs=in_specs, out_specs=out_specs, check_vma=False
    )
```

profile of v0, /device:TPU:0, one launch (start us, length us, event | category | flops | bytes accessed | tf_op | source)
XLA Modules:
  0.0 595.3 jit_solution(12372179383174552325)
XLA Ops:
  7.2 1.4 copy.36
  9.8 39.0 %fusion.79 = (f32[976]{0:T(1024)S(1)}, f32[976,768]{1,0:T(8,128)S(1)}) fusion(f32[768]{0:T(1024)} %param.26, bf16[3072,768]{1,0:T(8,128)(2,1)} %param.25, f32[3072]{0:T(1024)} %param.24, bf16[768,3072]{1,0:T(8,128)(2,1)} %param.23, bf16[720,768]{1,0:T(8,128)(2,1)} %reshape.220, bf16[256,768]{1,0:T(8,128)(2,1)} %bitcast.103), kind=kOutput, calls=%fused_computation.118 | convolution fusion | flops 9416821760 | bytes 13953856 | tf_op jit(solution)/shard_map/dot_general | solution.py:42
  53.0 159.0 %all-gather.2.cloned.1.call-done = bf16[256,32,129]{2,1,0:T(8,128)(2,1)} async-done(((bf16[8,32,129]{2,1,0:T(8,128)(2,1)}), bf16[256,32,129]{2,1,0:T(8,128)(2,1)}) %all-gather.2.cloned.1.call-update) | async-done | bytes 2113552 | tf_op jit(solution)/shard_map/all_gather | solution.py:19
  212.0 2.7 convert_reduce_fusion
  214.9 3.3 split.8
  218.2 31.5 %while.23 = (s32[]{:T(128)}, f32[16,16,4]{1,0,2:T(8,128)S(1)}, bf16[16,512,128]{2,1,0:T(8,128)(2,1)}, bf16[720,128]{1,0:T(8,128)(2,1)S(1)}, bf16[4,180]{1,0:T(4,...) while((s32[]{:T(128)}, f32[16,16,4]{1,0,2:T(8,128)S(1)}, bf16[16,512,128]{2,1,0:T(8,128)(2,1)}, ...), condition=%wide.region_6.7_spmd, body=%wide.region_3.6_spmd.sunk | while | flops 95480976 | bytes 6281597 | solution.py:155
  218.2 1.3 multiply_exponential_fusion.4
  220.1 1.3 multiply_exponential_fusion.4
  222.1 1.3 multiply_exponential_fusion.4
  224.1 1.3 multiply_exponential_fusion.4
  226.0 1.3 multiply_exponential_fusion.4
  228.0 1.3 multiply_exponential_fusion.4
  230.0 1.3 multiply_exponential_fusion.4
  232.0 1.3 multiply_exponential_fusion.4
  233.9 1.3 multiply_exponential_fusion.4
  235.9 1.3 multiply_exponential_fusion.4
  237.9 1.3 multiply_exponential_fusion.4
  239.8 1.3 multiply_exponential_fusion.4
  241.8 1.3 multiply_exponential_fusion.4
  243.8 1.3 multiply_exponential_fusion.4
  250.4 7.2 %all-to-all-start = ((f32[32,8,4]{1,2,0:T(4,128)}), f32[32,8,4]{1,2,0:T(4,128)S(1)}, u32[]{:S(2)}, u32[]{:S(2)}) async-start(f32[32,8,4]{1,2,0:T(4,128)} %copy.39), calls=%async_computation | async-start | bytes 131072 | tf_op jit(solution)/shard_map/all_to_all | solution.py:156
  257.7 8.3 %all-to-all-done = f32[32,8,4]{1,2,0:T(4,128)S(1)} async-done(((f32[32,8,4]{1,2,0:T(4,128)}), f32[32,8,4]{1,2,0:T(4,128)S(1)}, u32[]{:S(2)}, u32[]{:S(2)}) %all-to-all-start) | async-done | bytes 4128 | tf_op jit(solution)/shard_map/all_to_all | solution.py:156
  267.5 3.9 all-to-all-start.1
  271.4 8.3 %all-to-all-done.1 = f32[8,32,4]{0,2,1:T(4,128)S(1)} async-done(((f32[8,32,4]{0,2,1:T(4,128)}), f32[8,32,4]{0,2,1:T(4,128)S(1)}, u32[]{:S(2)}, u32[]{:S(2)}) %all-to-all-start.1) | async-done | bytes 4128 | tf_op jit(solution)/shard_map/all_to_all | solution.py:158
  279.7 134.8 %while.24 = (s32[]{:T(128)}, f32[4,180,128]{2,1,0:T(8,128)}, bf16[16,512,128]{2,1,0:T(8,128)(2,1)}, bf16[16,512,128]{2,1,0:T(8,128)(2,1)}, bf16[720,128]{1,0:T(8...) while((s32[]{:T(128)}, f32[4,180,128]{2,1,0:T(8,128)}, ...), condition=%wide.region_13.14_spmd.clone, body=%wide.region_11.13_spmd.clone.sunk | while | flops 285514432 | bytes 21625324 | solution.py:170
  283.1 1.7 multiply_convert_fusion.3
  286.0 1.3 convolution_add_fusion.2
  291.5 1.7 multiply_convert_fusion.3
  294.5 1.3 convolution_add_fusion.2
  300.0 1.7 multiply_convert_fusion.3
  302.9 1.3 convolution_add_fusion.2
  308.4 1.7 multiply_convert_fusion.3
  311.3 1.3 convolution_add_fusion.2
  316.8 1.7 multiply_convert_fusion.3
  319.7 1.3 convolution_add_fusion.2
  325.2 1.7 multiply_convert_fusion.3
  328.2 1.3 convolution_add_fusion.2
  333.6 1.7 multiply_convert_fusion.3
  336.6 1.3 convolution_add_fusion.2
  342.1 1.7 multiply_convert_fusion.3
  345.0 1.3 convolution_add_fusion.2
  350.5 1.7 multiply_convert_fusion.3
  353.4 1.3 convolution_add_fusion.2
  358.9 1.7 multiply_convert_fusion.3
  361.9 1.3 convolution_add_fusion.2
  367.4 1.7 multiply_convert_fusion.3
  370.3 1.3 convolution_add_fusion.2
  375.8 1.7 multiply_convert_fusion.3
  378.7 1.3 convolution_add_fusion.2
  384.2 1.7 multiply_convert_fusion.3
  387.1 1.3 convolution_add_fusion.2
  392.6 1.7 multiply_convert_fusion.3
  395.6 1.3 convolution_add_fusion.2
  401.0 1.7 multiply_convert_fusion.3
  404.0 1.3 convolution_add_fusion.2
  409.5 1.7 multiply_convert_fusion.3
  412.4 1.3 convolution_add_fusion.2
  414.5 4.9 all-to-all-start.2
  421.0 17.0 %all-to-all-done.2 = bf16[32,8,32,128]{3,2,1,0:T(8,128)(2,1)} async-done(((bf16[32,8,32,128]{3,2,1,0:T(8,128)(2,1)}), bf16[32,8,32,128]{3,2,1,0:T(8,128)(2,1)}, u32[]{:S(2)}, u32[]{:S(2)}) %all-to-all-start.2) | async-done | bytes 2097184 | tf_op jit(solution)/shard_map/all_to_all | solution.py:31
  438.0 1.9 convert_reduce_fusion.1
  440.2 1.4 fusion.32
  441.6 62.9 %psum.14 = f32[]{:T(128)} all-reduce(f32[]{:T(128)} %get-tuple-element.186), channel_id=1, replica_groups=mesh['rep'=4,'dp'=32] {'rep','dp'}, use_global_device_ids=true, to_apply=%region_10.11 | all-reduce | flops 1 | bytes 8 | tf_op jit(solution)/shard_map/psum | solution.py:185
  506.0 79.6 %all-reduce.2.cloned.1.call-done = f32[768,128]{1,0:T(8,128)} async-done(((f32[768,128]{1,0:T(8,128)}), f32[768,128]{1,0:T(8,128)}) %all-reduce.2.cloned.1.call-update) | async-done | bytes 393232 | tf_op jit(solution)/shard_map/psum | solution.py:185
  585.6 1.8 copy.73
  (499 shorter events, 107.8 us)
Async XLA Ops:
  7.2 43.9 %copy-start = (bf16[768,128]{1,0:T(8,128)(2,1)S(1)}, bf16[768,128]{1,0:T(8,128)(2,1)}, u32[]{:S(2)}) copy-start(bf16[768,128]{1,0:T(8,128)(2,1)} %param.29) | copy-start | bytes 589828
  7.2 204.8 %all-gather.2.cloned.1.call-start = ((), (), s32[]{:S(2)}) async-start(), calls=%async_computation.3 | async-start | bytes 4325376 | tf_op jit(solution)/shard_map/all_gather | solution.py:19
  9.7 39.6 %copy-start.10 = (f32[768]{0:T(1024)S(1)}, f32[768]{0:T(1024)}, u32[]{:S(2)}) copy-start(f32[768]{0:T(1024)} %param.28) | copy-start | bytes 9220
  9.8 39.6 %copy-start.11 = (f32[768]{0:T(1024)S(1)}, f32[768]{0:T(1024)}, u32[]{:S(2)}) copy-start(f32[768]{0:T(1024)} %param.27) | copy-start | bytes 9220
  48.8 3.1 copy-start.13
  49.3 3.6 copy-start.9
  49.3 3.6 copy-start.14
  49.9 1.1 copy-start.4
  51.7 367.8 %copy-start.8 = (f32[976]{0:T(1024)}, f32[976]{0:T(1024)S(1)}, u32[]{:S(2)}) copy-start(f32[976]{0:T(1024)S(1)} %add_rsqrt_fusion) | copy-start | bytes 11716
  51.9 166.2 %copy-start.6 = (f32[976,128]{1,0:T(8,128)}, f32[976,128]{1,0:T(8,128)S(1)}, u32[]{:S(2)}) copy-start(f32[976,128]{1,0:T(8,128)S(1)} %broadcast_multiply_fusion) | copy-start | bytes 1499140
  218.2 47.9 %copy-start.12 = (s32[8]{0:T(128)S(1)}, s32[8]{0:T(128)}, u32[]{:S(2)}) copy-start(s32[8]{0:T(128)} %param.22) | copy-start | bytes 100
  250.4 15.6 %all-to-all-start = ((f32[32,8,4]{1,2,0:T(4,128)}), f32[32,8,4]{1,2,0:T(4,128)S(1)}, u32[]{:S(2)}, u32[]{:S(2)}) async-start(f32[32,8,4]{1,2,0:T(4,128)} %copy.39), calls=%async_computation | async-start | bytes 131072 | tf_op jit(solution)/shard_map/all_to_all | solution.py:156
  267.5 12.2 %all-to-all-start.1 = ((f32[8,32,4]{0,2,1:T(4,128)}), f32[8,32,4]{0,2,1:T(4,128)S(1)}, u32[]{:S(2)}, u32[]{:S(2)}) async-start(f32[8,32,4]{0,2,1:T(4,128)} %fusion.40), calls=%async_computation.1 | async-start | bytes 131072 | tf_op jit(solution)/shard_map/all_to_all | solution.py:158
  283.0 3.0 copy-start.1
  287.4 0.8 copy-start.2
  291.4 3.0 copy-start.1
  295.8 0.8 copy-start.2
  299.9 3.0 copy-start.1
  304.2 0.8 copy-start.2
  308.3 3.0 copy-start.1
  312.7 0.8 copy-start.2
  316.7 3.0 copy-start.1
  321.1 0.8 copy-start.2
  325.1 3.0 copy-start.1
  329.5 0.8 copy-start.2
  333.6 3.0 copy-start.1
  337.9 0.8 copy-start.2
  342.0 3.0 copy-start.1
  346.4 0.8 copy-start.2
  350.4 3.0 copy-start.1
  354.8 0.8 copy-start.2
  358.8 3.0 copy-start.1
  363.2 0.8 copy-start.2
  367.3 3.0 copy-start.1
  371.6 0.8 copy-start.2
  375.7 3.0 copy-start.1
  380.1 0.8 copy-start.2
  384.1 3.0 copy-start.1
  388.5 0.8 copy-start.2
  392.5 3.0 copy-start.1
  396.9 0.8 copy-start.2
  401.0 3.0 copy-start.1
  405.3 0.8 copy-start.2
  409.4 3.0 copy-start.1
  413.7 0.8 copy-start.2
  414.5 6.1 %copy-start.7 = (f32[976,128]{1,0:T(8,128)S(1)}, f32[976,128]{1,0:T(8,128)}, u32[]{:S(2)}) copy-start(f32[976,128]{1,0:T(8,128)} %copy-done.6) | copy-start | bytes 1499140
  414.5 25.7 %copy-start.5 = (bf16[976,768]{1,0:T(8,128)(2,1)S(1)}, bf16[976,768]{1,0:T(8,128)(2,1)}, u32[]{:S(2)}) copy-start(bf16[976,768]{1,0:T(8,128)(2,1)} %copy-done.4) | copy-start | bytes 4497412
  414.5 23.5 %all-to-all-start.2 = ((bf16[32,8,32,128]{3,2,1,0:T(8,128)(2,1)}), bf16[32,8,32,128]{3,2,1,0:T(8,128)(2,1)}, u32[]{:S(2)}, u32[]{:S(2)}) async-start(bf16[32,8,32,128]{3,2,1,0:T(8,128)(2,1)} %bitcast.97), calls=%async_computation.2 | async-start | bytes 4194304 | tf_op jit(solution)/shard_map/all_to_all | solution.py:31
  419.4 85.7 %copy-start.3 = (f32[4,180,128]{2,1,0:T(8,128)S(1)}, f32[4,180,128]{2,1,0:T(8,128)}, u32[]{:S(2)}) copy-start(f32[4,180,128]{2,1,0:T(8,128)} %get-tuple-element.153) | copy-start | bytes 1105924
  419.4 166.1 %all-reduce.2.cloned.1.call-start = ((), (), s32[]{:S(2)}) async-start(), calls=%async_computation.4 | async-start | bytes 786432 | tf_op jit(solution)/shard_map/psum | solution.py:185
  419.5 20.5 %slice-start = ((f32[976]{0:T(1024)}), f32[256]{0:T(256)S(1)}, s32[]{:S(2)}) async-start(f32[976]{0:T(1024)} %copy-done.8), calls=%async_computation.5 | async-start | bytes 2048 | tf_op jit(solution)/shard_map/slice | solution.py:177
Sparse Core Ops, SparseCore 0:
  53.0 158.9 all-gather.1
  441.7 143.8 all-reduce.1
where the time goes:
time: 598 us; the launch traced here: 595 us
  waiting for transfers between devices  272 us (45%)
  matrix products  120 us (20%)
  blocking collectives  62.9 us (11%)
  local copies, waits for them, and re-layouts  61.1 us (10%)
  other arithmetic  44.3 us (7%)
  starting transfers between devices  16.1 us (3%)
  between operations  16.1 us (3%)
    all_gather x1, waiting for transfers between devices, in_one_piece(): out = lax.all_gather(both, axis, axis=dim, tiled=True)  159 us
    psum x1, waiting for transfers between devices, per_device(): proj_total, loss_total = lax.psum((local_sum, loss_sum), ('rep', 'dp'))  79.6 us
    psum x1, blocking collectives, per_device(): proj_total, loss_total = lax.psum((local_sum, loss_sum), ('rep', 'dp'))  62.9 us
    dot_general x32, matrix products, token_scores(): lax.dot_general(query_flat, flat_block, (((1,), (1,)), ((), ())), preferr...  40.4 us
    dot_general x1, matrix products, encode_rows(): jnp.dot(activated, down_weight, preferred_element_type=jnp.float32)  39 us
    convert_element_type x16, other arithmetic, token_grads(): (weights * factor[:, :, None]).reshape(-1, item_count * pass_len)  27.2 us
    mul x32, local copies, waits for them, and re-layouts, token_grads(): weights * factor[:, :, None]  23 us
    dot_general x16, matrix products, token_grads(): lax.dot_general(sim_grad, query_flat, (((0,), (0,)), ((), ())), preferred...  21.4 us
  transfers between devices with their start and end apart: 5, of which 5 were waited for; matrix products, arithmetic and copies ran while one was open for 0% of the time, Pallas kernels for 0%

commit v1 on v0

v1 whole, which is shorter than its diff:
```python
import functools
import math

import jax
import jax.numpy as jnp
from jax import lax
from jax.experimental import pallas as pl
from jax.experimental.pallas import tpu as pltpu
from jax.sharding import PartitionSpec as P

temper = 0.05
eps_norm = 1e-06
punct_low = 999
punct_high = 1067
MESH = pl.DeviceIdType.MESH
bf16 = jnp.bfloat16
f32 = jnp.float32

QD, QL, PD, PLN, D, FF, E = 8, 32, 4, 180, 768, 3072, 128
QT = QD * QL
PP = 192
ZX = 16
YC = 8
HALF = PD * PP
DW = 768
CW = 512
CH = D // ZX


def butterfly(x, lane):
    for k in (1, 2, 4, 8, 16):
        up = pltpu.roll(x, k, 1)
        down = pltpu.roll(x, 128 - k, 1)
        x = x + jnp.where((lane & k) != 0, up, down)
    return x


def kernel(
    qs, ps, qlen, plen, ids, pos, upw, upb, dnw, dnb, gain, bias, pw,
    loss_out, pg_out, gr_out,
    xq, xs, wup, wdn, acc, hid, nrm, inv, qall, pall, ptr, axo, axall, kpo, kpr, keepm,
    wts, tot, scr, onh, fac, msg, sg, pgacc, qg, qr, psend, precv, pgo, back, grad, rs, mids, midr, fin,
    ld_sem, up_sem, dn_sem, q_ss, q_rs, a_ss, a_rs, k_sem, p_ss, p_rs, m_ss, m_rs,
    g_ss, g_rs, pg_sem, r_ss, r_rs, c_ss, c_rs, f_ss, f_rs, o_sem,
):
    rep, dp = lax.axis_index("rep"), lax.axis_index("dp")
    y, zx = lax.div(dp, ZX), lax.rem(dp, ZX)
    z, x = lax.div(zx, 4), lax.rem(zx, 4)
    other = lax.rem(dp + ZX, 2 * ZX)
    col = rep * 2 + y

    def member(k):
        return lax.rem(z + lax.div(k, 4), 4) * 4 + lax.rem(x + lax.rem(k, 4), 4)

    def source(k):
        return lax.rem(z + 4 - lax.div(k, 4), 4) * 4 + lax.rem(x + 4 - lax.rem(k, 4), 4)

    def row_dev(m):
        return (rep, y * ZX + m)

    def col_dev(m):
        return (lax.div(m, 2), lax.rem(m, 2) * ZX + zx)

    def remote(src, dst, ss, rs_, dev):
        return pltpu.make_async_remote_copy(
            src_ref=src, dst_ref=dst, send_sem=ss, recv_sem=rs_, device_id=dev, device_id_type=MESH
        )

    load_q = pltpu.make_async_copy(qs, xq, ld_sem.at[0])
    load_p = pltpu.make_async_copy(ps, xs, ld_sem.at[1])
    ups = [
        pltpu.make_async_copy(upw.at[:, pl.ds(c * DW, DW)], wup.at[:, pl.ds(c * DW, DW)], up_sem.at[c])
        for c in range(FF // DW)
    ]
    dns = [
        pltpu.make_async_copy(dnw.at[pl.ds(c * DW, DW)], wdn.at[pl.ds(c * DW, DW)], dn_sem.at[c])
        for c in range(FF // DW)
    ]
    load_q.start()
    for c in range(FF // DW):
        ups[c].start()
        dns[c].start()
    load_p.start()

    barrier = pltpu.get_barrier_semaphore()

    @pl.loop(1, ZX)
    def _(k):
        pl.semaphore_signal(barrier, inc=1, device_id=row_dev(member(k)), device_id_type=MESH)

    @pl.loop(1, YC)
    def _(k):
        pl.semaphore_signal(barrier, inc=1, device_id=col_dev(lax.rem(col + k, YC)), device_id_type=MESH)

    lane = lax.broadcasted_iota(jnp.int32, (8, 128), 1)
    row8 = lax.broadcasted_iota(jnp.int32, (8, 128), 0)
    for c in range(2):
        qn = lax.shift_right_logical(lane, 5) + 4 * c
        lens = jnp.zeros((8, 128), jnp.int32)
        posv = jnp.zeros((8, 128), jnp.int32)
        for n in range(4 * c, 4 * c + 4):
            lens = jnp.where(qn == n, qlen[n], lens)
            posv = jnp.where(qn == n, pos[n], posv)
        keep = ((lane & 31) < lens).astype(f32)
        axo[c] = jnp.where(row8 == 0, keep, posv.astype(f32))
    axall[zx] = axo[...]
    kpo[...] = jnp.zeros(kpo.shape, f32)
    tcol = lax.broadcasted_iota(jnp.int32, (PD, PLN), 1)
    prow = lax.broadcasted_iota(jnp.int32, (PD, PLN), 0)
    plens = jnp.zeros((PD, PLN), jnp.int32)
    for k in range(PD):
        plens = jnp.where(prow == k, plen[k], plens)
    idv = ids[...]
    good = (tcol < plens) & ((idv < punct_low) | (idv >= punct_high))
    kpo[0:PD, 0:PLN] = good.astype(f32)

    hid[...] = jnp.zeros(hid.shape, bf16)
    back[...] = jnp.zeros(back.shape, bf16)
    pall[0:PD] = jnp.zeros((PD, PP, E), bf16)
    pgacc[...] = jnp.zeros(pgacc.shape, f32)

    def feed(xref, rows, wait):
        for c in range(FF // CW):
            wait(c)
            cs = slice(c * CW, (c + 1) * CW)
            up = jnp.dot(xref[...], wup[:, cs], preferred_element_type=f32) + upb[:, cs]
            act = ((0.5 * up) * (1.0 + lax.erf(up * (1.0 / math.sqrt(2.0))))).astype(bf16)
            part = jnp.dot(act, wdn[cs, :], preferred_element_type=f32)
            if c == 0:
                acc[0:rows, :] = part + (xref[...].astype(f32) + dnb[...])
            else:
                acc[0:rows, :] += part

    def finish(rows):
        res = acc[0:rows, :]
        cen = res - jnp.mean(res, -1, keepdims=True)
        var = jnp.mean(cen * cen, -1, keepdims=True)
        h = (cen * lax.rsqrt(var + eps_norm) * gain[...] + bias[...]).astype(bf16)
        proj = jnp.dot(h, pw[...], preferred_element_type=f32)
        iv = lax.rsqrt(jnp.sum(proj * proj, -1, keepdims=True) + eps_norm)
        return h, proj * iv, jnp.broadcast_to(iv, proj.shape)

    load_q.wait()
    waited = set()

    def wait_weights(c):
        for part in range((c * CW) // DW, ((c + 1) * CW - 1) // DW + 1):
            if part not in waited:
                waited.add(part)
                ups[part].wait()
                dns[part].wait()

    feed(xq, QT, wait_weights)
    h, n, iv = finish(QT)
    hid[0:QT, :] = h
    nrm[0:QT, :] = n
    inv[0:QT, :] = iv
    qall[zx] = n.astype(bf16)

    pl.semaphore_wait(barrier, ZX - 1 + YC - 1)

    def q_copy(slot, m):
        return remote(qall.at[slot], qall.at[slot], q_ss.at[m], q_rs.at[slot], row_dev(m))

    def a_copy(slot, m):
        return remote(axall.at[slot], axall.at[slot], a_ss.at[m], a_rs.at[slot], row_dev(m))

    @pl.loop(1, ZX)
    def _(k):
        m = member(k)
        q_copy(zx, m).start()
        a_copy(zx, m).start()

    k_copy = remote(kpo.at[pl.ds(0, 8)], kpr.at[pl.ds(0, 8)], k_sem.at[0], k_sem.at[1], (rep, other))
    k_copy.start()

    load_p.wait()

    def p_copy(k):
        return remote(pall.at[k], pall.at[PD + k], p_ss.at[k], p_rs.at[k], (rep, other))

    @pl.loop(0, PD)
    def _(k):
        feed(xs.at[k], PLN, lambda c: None)
        h, n, iv = finish(PLN)
        at = pl.multiple_of(QT + k * PP, 64)
        hid[pl.ds(at, PLN), :] = h
        nrm[pl.ds(at, PLN), :] = n
        inv[pl.ds(at, PLN), :] = iv
        pall[k, 0:PLN, :] = n.astype(bf16)
        p_copy(k).start()

    def make_masks(src, base):
        v = jnp.transpose(src[...])
        for k in range(PD):
            keepm[base + k] = jnp.broadcast_to(v[0:PP, k : k + 1], (PP, 128))

    def make_ptr(h):
        v = pall[h * PD : (h + 1) * PD].reshape(HALF, E).astype(f32)
        ptr[:, h * HALF : (h + 1) * HALF] = jnp.transpose(v).astype(bf16)

    scale = math.log2(math.e) / temper

    def forward(j, h):
        q = qall[j]
        for k in range(PD):
            p = h * PD + k
            s = lax.dot_general(pall[p], q, (((1,), (1,)), ((), ())), preferred_element_type=f32)
            km = keepm[p]
            for c in range(2):
                w = jnp.exp2(s[:, c * 128 : (c + 1) * 128] * scale) * km
                wts[j, p * PP : (p + 1) * PP, c * 128 : (c + 1) * 128] = w
                tot[j, c, p : p + 1, :] = jnp.sum(w, axis=0, keepdims=True)

    make_masks(kpo, 0)
    make_ptr(0)

    @pl.loop(0, ZX)
    def _(k):
        j = source(k)

        @pl.when(k > 0)
        def _():
            q_copy(j, j).wait_recv()
            a_copy(j, j).wait_recv()

        forward(j, 0)

    k_copy.wait_recv()
    for k in range(PD):
        p_copy(k).wait_recv()
    make_masks(kpr, PD)
    make_ptr(1)

    @pl.loop(0, ZX)
    def _(k):
        forward(k, 1)

    shape4 = (ZX, 2, 8, 128)
    lane2 = lax.broadcasted_iota(jnp.int32, (ZX * 2 * 8, 128), 1)
    keepq = axall[:, :, 0:1, :]
    posq = axall[:, :, 1:2, :]
    tv = tot[...]
    soft = temper * jnp.log(tv) * keepq
    s2 = butterfly(soft.reshape(ZX * 2 * 8, 128), lane2)
    s4 = s2.reshape(shape4)
    pidx = lax.broadcasted_iota(jnp.int32, shape4, 2)
    pid = jnp.where(pidx < PD, dp * PD + pidx, other * PD + pidx - PD).astype(f32)
    one = (jnp.broadcast_to(posq, shape4) == pid).astype(f32)
    pick = (lax.broadcasted_iota(jnp.int32, shape4, 3) & 31) == (
        lax.broadcasted_iota(jnp.int32, shape4, 0) * 2 + lax.broadcasted_iota(jnp.int32, shape4, 1)
    )
    se = jnp.sum(jnp.sum(jnp.where(pick, jnp.exp(s4), 0.0), axis=(0, 1)), axis=0, keepdims=True)
    po = jnp.sum(jnp.sum(jnp.where(pick, s4 * one, 0.0), axis=(0, 1)), axis=0, keepdims=True)
    msg[zx] = jnp.where(row8 == 0, se, jnp.where(row8 == 1, po, 0.0))
    scr[...] = s4
    onh[...] = one

    def m_copy(slot, m):
        return remote(msg.at[slot], msg.at[slot], m_ss.at[m], m_rs.at[slot], row_dev(m))

    @pl.loop(1, ZX)
    def _(k):
        m_copy(zx, member(k)).start()

    @pl.loop(1, ZX)
    def _(k):
        j = source(k)
        m_copy(j, j).wait_recv()

    both = jnp.sum(msg[...], axis=0)
    lt = jnp.log(both[0:1, :])
    loss_row = jnp.sum(lt - both[1:2, :], axis=1, keepdims=True)
    lx = butterfly(
        jnp.where(pick, jnp.broadcast_to(lt.reshape(1, 1, 1, 128), shape4), 0.0).reshape(ZX * 2 * 8, 128), lane2
    ).reshape(shape4)
    dsc = jnp.exp(scr[...] - lx) - onh[...]
    fac[...] = (dsc * axall[:, :, 0:1, :]) / tot[...]

    def g_copy(src, dst, m):
        return remote(qg.at[src], qr.at[dst], g_ss.at[src], g_rs.at[dst], row_dev(m))

    @pl.loop(0, ZX)
    def _(k0):
        k = lax.rem(k0 + 1, ZX)
        j = member(k)
        q = qall[j]
        for p in range(2 * PD):
            f = jnp.concatenate([fac[j, 0, p : p + 1, :], fac[j, 1, p : p + 1, :]], axis=1)
            sg[p * PP : (p + 1) * PP, :] = (wts[j, p * PP : (p + 1) * PP, :] * f).astype(bf16)
        for h in range(2):
            hs = slice(h * HALF, (h + 1) * HALF)
            pgacc[hs, :] += jnp.dot(sg[hs, :], q, preferred_element_type=f32)
        qg[j] = jnp.dot(ptr[...], sg[...], preferred_element_type=f32).astype(bf16)

        @pl.when(k > 0)
        def _():
            g_copy(j, zx, j).start()

        @pl.when(k == 0)
        def _():
            qr[zx] = qg[j]

    psend[...] = pgacc[HALF:, :].astype(bf16)
    pg_copy = remote(psend, precv, pg_sem.at[0], pg_sem.at[1], (rep, other))
    pg_copy.start()
    pg_copy.wait_recv()

    def backward(g, at, rows):
        n = nrm[at : at + rows, :]
        return (inv[at : at + rows, :] * (g - n * jnp.sum(n * g, -1, keepdims=True))).astype(bf16)

    for k in range(PD):
        g = pgacc[k * PP : k * PP + PLN, :] + precv[k * PP : k * PP + PLN, :].astype(f32)
        pgo[k] = g
        back[QT + k * PP : QT + k * PP + PLN, :] = backward(g, QT + k * PP, PLN)
    out_copy = pltpu.make_async_copy(pgo, pg_out, o_sem)
    out_copy.start()

    @pl.loop(1, ZX)
    def _(k):
        j = source(k)
        g_copy(j, j, j).wait_recv()

    qsum = jnp.sum(qr[...].astype(f32), axis=0)
    back[0:QT, :] = backward(jnp.transpose(qsum), 0, QT)
    gt = lax.dot_general(back[...], hid[...], (((0,), (0,)), ((), ())), preferred_element_type=f32)
    grad[...] = jnp.transpose(gt)

    def r_copy(src, dst, m):
        return remote(grad.at[pl.ds(src * CH, CH)], rs.at[dst], r_ss.at[src], r_rs.at[dst], row_dev(m))

    @pl.loop(1, ZX)
    def _(k):
        m = member(k)
        r_copy(m, zx, m).start()

    rs[zx] = grad[pl.ds(pl.multiple_of(zx * CH, 8), CH), :]

    @pl.loop(1, ZX)
    def _(k):
        j = source(k)
        r_copy(j, j, j).wait_recv()

    mids[0:CH, :] = jnp.sum(rs[...], axis=0)
    mids[CH : CH + 8, :] = jnp.broadcast_to(loss_row, (8, 128))

    def c_copy(dst, m):
        return remote(mids, midr.at[dst], c_ss.at[m], c_rs.at[dst], col_dev(m))

    @pl.loop(1, YC)
    def _(k):
        c_copy(col, lax.rem(col + k, YC)).start()

    midr[col] = mids[...]

    @pl.loop(1, YC)
    def _(k):
        m = lax.rem(col + k, YC)
        c_copy(m, m).wait_recv()

    whole = jnp.sum(midr[...], axis=0)
    loss_out[...] = whole[CH:, :] * (1.0 / 1024.0)
    mine = pl.ds(pl.multiple_of(zx * CH, 8), CH)
    gr_out[mine, :] = whole[0:CH, :]

    def f_copy(slot, m):
        rows = pl.ds(pl.multiple_of(slot * CH, 8), CH)
        return remote(gr_out.at[rows], gr_out.at[rows], f_ss.at[m], f_rs.at[slot], row_dev(m))

    @pl.loop(1, ZX)
    def _(k):
        f_copy(zx, member(k)).start()

    @pl.loop(1, ZX)
    def _(k):
        j = source(k)
        f_copy(j, j).wait_recv()

    @pl.loop(1, ZX)
    def _(k):
        m = member(k)
        q_copy(zx, m).wait_send()
        a_copy(zx, m).wait_send()
        m_copy(zx, m).wait_send()
        g_copy(m, zx, m).wait_send()
        r_copy(m, zx, m).wait_send()
        f_copy(zx, m).wait_send()

    @pl.loop(1, YC)
    def _(k):
        c_copy(col, lax.rem(col + k, YC)).wait_send()

    k_copy.wait_send()
    for k in range(PD):
        p_copy(k).wait_send()
    pg_copy.wait_send()
    out_copy.wait()


def per_device(qs, ps, qlen, plen, ids, pos, upw, upb, dnw, dnb, gain, bias, pw):
    anyspace = pl.BlockSpec(memory_space=pl.ANY)
    vm = pl.BlockSpec(memory_space=pltpu.VMEM)
    sm = pl.BlockSpec(memory_space=pltpu.SMEM)
    dma = pltpu.SemaphoreType.DMA
    loss, pgrad, grad = pl.pallas_call(
        kernel,
        name="step",
        out_shape=(
            jax.ShapeDtypeStruct((8, 128), f32),
            jax.ShapeDtypeStruct((PD, PLN, E), f32),
            jax.ShapeDtypeStruct((D, E), f32),
        ),
        in_specs=[anyspace, anyspace, sm, sm, vm, sm, anyspace, vm, anyspace, vm, vm, vm, vm],
        out_specs=(vm, anyspace, vm),
        scratch_shapes=[
            pltpu.VMEM((QT, D), bf16),
            pltpu.VMEM((PD, PLN, D), bf16),
            pltpu.VMEM((D, FF), bf16),
            pltpu.VMEM((FF, D), bf16),
            pltpu.VMEM((QT, D), f32),
            pltpu.VMEM((QT + HALF, D), bf16),
            pltpu.VMEM((QT + HALF, E), f32),
            pltpu.VMEM((QT + HALF, E), f32),
            pltpu.VMEM((ZX, QT, E), bf16),
            pltpu.VMEM((2 * PD, PP, E), bf16),
            pltpu.VMEM((E, 2 * HALF), bf16),
            pltpu.VMEM((2, 8, 128), f32),
            pltpu.VMEM((ZX, 2, 8, 128), f32),
            pltpu.VMEM((128, 256), f32),
            pltpu.VMEM((128, 256), f32),
            pltpu.VMEM((2 * PD, PP, 128), f32),
            pltpu.VMEM((ZX, 2 * HALF, QT), f32),
            pltpu.VMEM((ZX, 2, 8, 128), f32),
            pltpu.VMEM((ZX, 2, 8, 128), f32),
            pltpu.VMEM((ZX, 2, 8, 128), f32),
            pltpu.VMEM((ZX, 2, 8, 128), f32),
            pltpu.VMEM((ZX, 8, 128), f32),
            pltpu.VMEM((2 * HALF, QT), bf16),
            pltpu.VMEM((2 * HALF, E), f32),
            pltpu.VMEM((ZX, E, QT), bf16),
            pltpu.VMEM((ZX, E, QT), bf16),
            pltpu.VMEM((HALF, E), bf16),
            pltpu.VMEM((HALF, E), bf16),
            pltpu.VMEM((PD, PLN, E), f32),
            pltpu.VMEM((QT + HALF, E), bf16),
            pltpu.VMEM((D, E), f32),
            pltpu.VMEM((ZX, CH, E), f32),
            pltpu.VMEM((CH + 8, E), f32),
            pltpu.VMEM((YC, CH + 8, E), f32),
            pltpu.VMEM((8, 128), f32),
            dma((2,)), dma((4,)), dma((4,)),
            dma((ZX,)), dma((ZX,)), dma((ZX,)), dma((ZX,)),
            dma((2,)), dma((PD,)), dma((PD,)), dma((ZX,)), dma((ZX,)),
            dma((ZX,)), dma((ZX,)), dma((2,)), dma((ZX,)), dma((ZX,)),
            dma((YC,)), dma((YC,)), dma((ZX,)), dma((ZX,)), dma,
        ],
        compiler_params=pltpu.CompilerParams(
            collective_id=0, has_side_effects=True, vmem_limit_bytes=60 * 1024 * 1024
        ),
    )(
        qs.reshape(QT, D), ps, qlen, plen, ids, pos, upw, upb.reshape(1, FF), dnw, dnb.reshape(1, D),
        gain.reshape(1, D), bias.reshape(1, D), pw,
    )
    return loss[0, 0], pgrad, grad


def solution(mesh):
    both = ("rep", "dp")
    in_specs = (
        P(both, None, None), P(both, None, None), P(both), P(both), P(both, None), P(both),
        P(), P(), P(), P(), P(), P(), P(),
    )
    out_specs = (P(), P(both, None, None), P())
    return jax.shard_map(per_device, mesh=mesh, in_specs=in_specs, out_specs=out_specs, check_vma=False)
```

time: 598 us -> 95.3 us (0.16)
  waiting for transfers between devices: 272 us -> 0 us
  matrix products: 120 us -> 0 us
  Pallas kernels: 0 us -> 83.4 us
  blocking collectives: 62.9 us -> 0 us
  local copies, waits for them, and re-layouts: 61.1 us -> 10.9 us
  other arithmetic: 44.3 us -> 0 us
  starting transfers between devices: 16.1 us -> 0 us
  between operations: 16.1 us -> 0.64 us
    all_gather x1 -> x0, waiting for transfers between devices: 159 us -> none  [in_one_piece(): out = lax.all_gather(both, axis, axis=dim, tiled=True)]
    dot_general x67 -> x0, matrix products: 120 us -> none  [the longest x32 40.4 us: token_scores(): lax.dot_general(query_flat, flat_block, (((1,), (1,)), ((), ())), preferr...]
    pallas_call x0 -> x1, Pallas kernels: none -> 83.4 us  [per_device(): pl.pallas_call(kernel, name='step', out_shape=(jax.ShapeDtypeStruct((8, 1...]
    psum x1 -> x0, waiting for transfers between devices: 79.6 us -> none  [per_device(): proj_total, loss_total = lax.psum((local_sum, loss_sum), ('rep', 'dp'))]
    psum x1 -> x0, blocking collectives: 62.9 us -> none  [per_device(): proj_total, loss_total = lax.psum((local_sum, loss_sum), ('rep', 'dp'))]
    all_to_all x3 -> x0, waiting for transfers between devices: 33.6 us -> none  [the longest x1 17 us: summed_on_arrival(): lax.all_to_all(blocks, axis, split_axis=0, concat_axis=0, tiled=True)]
    convert_element_type x54 -> x0, other arithmetic: 31.1 us -> none  [the longest x16 27.2 us: token_grads(): (weights * factor[:, :, None]).reshape(-1, item_count * pass_len)]
    mul x80 -> x0, local copies, waits for them, and re-layouts: 26.7 us -> none  [the longest x32 23 us: token_grads(): weights * factor[:, :, None]]
  transfers between devices with their start and end apart: 5 -> 0, of which waited for: 5 -> 0; matrix products, arithmetic and copies ran while one was open for 0% -> 0% of each run, Pallas kernels for 0% -> 0%
where the time goes in v1:
time: 95.3 us; the launch traced here: 94.9 us
  Pallas kernels  83.4 us (88%)
  local copies, waits for them, and re-layouts  10.9 us (11%)
    pallas_call x1, Pallas kernels, per_device(): pl.pallas_call(kernel, name='step', out_shape=(jax.ShapeDtypeStruct((8, 1...  83.4 us
    unnamed x3, local copies, waits for them, and re-layouts  5.95 us

profile of v1, /device:TPU:0, one launch (start us, length us, event | category | flops | bytes accessed | tf_op | source)
XLA Modules:
  0.0 94.9 jit_solution(1903515632399474351)
XLA Ops:
  0.6 1.3 %reshape.23.dnb = f32[1,768]{1,0:T(1,128)} reshape(f32[768]{0:T(1024)} %param.22) | data formatting | bytes 6144 | tf_op jit(solution)/shard_map/reshape | solution.py:462
  1.9 1.3 %reshape.24.gain = f32[1,768]{1,0:T(1,128)} reshape(f32[768]{0:T(1024)} %param.23) | data formatting | bytes 6144 | tf_op jit(solution)/shard_map/reshape | solution.py:463
  3.2 1.3 %reshape.25.bias = f32[1,768]{1,0:T(1,128)} reshape(f32[768]{0:T(1024)} %param.24) | data formatting | bytes 6144 | tf_op jit(solution)/shard_map/reshape | solution.py:463
  4.4 2.4 %copy.16.ps = bf16[4,180,768]{2,1,0:T(8,128)(2,1)} copy(bf16[4,180,768]{2,0,1:T(4,128)(2,1)} %param.14) | data formatting | bytes 2211840 | tf_op args[1]
  6.8 83.4 %step.1 = (f32[8,128]{1,0:T(8,128)}, f32[4,180,128]{2,1,0:T(8,128)}, f32[768,128]{1,0:T(8,128)}) custom-call(bf16[256,768]{1,0:T(8,128)(2,1)} %bitcast.3, bf16[4,180,768]{2,1,0:T(8,128)(2,1)} %copy.16.ps, s32[8]{0:T(128)} %qlen.1, s32[4]{0:T(128)} %plen.1, s32[4,180]{1,0:T(4,128)} %ids.1, s32[8]{0:T(128)} %pos.1, bf16[768,3072]{1,0:T(8,128)(2,1)} %upw.1, ...), custom_call_target="tpu_custom_call" | custom-call | tf_op jit(solution)/shard_map/step/pallas_call | solution.py:406
  90.2 1.2 %slice.3 = f32[1,1]{1,0:T(1,128)} slice(f32[8,128]{1,0:T(8,128)} %get-tuple-element.6), slice={[0:1], [0:1]} | slice | bytes 8 | tf_op jit(solution)/shard_map/slice | solution.py:465
  91.4 1.8 %copy.17 = f32[4,180,128]{2,0,1:T(4,128)} copy(f32[4,180,128]{2,1,0:T(8,128)} %get-tuple-element.10) | data formatting | bytes 737280
  93.2 1.8 %copy.19 = f32[768,128]{1,0:T(8,128)} copy(f32[768,128]{1,0:T(8,128)} %get-tuple-element.17) | data formatting | bytes 786432

commit v2 on v1

v2 whole, which is shorter than its diff:
```python
import functools
import math

import jax
import jax.numpy as jnp
from jax import lax
from jax.experimental import pallas as pl
from jax.experimental.pallas import tpu as pltpu
from jax.sharding import PartitionSpec as P

temper = 0.05
eps_norm = 1e-06
punct_low = 999
punct_high = 1067
MESH = pl.DeviceIdType.MESH
bf16 = jnp.bfloat16
f32 = jnp.float32

QD, QL, PD, PLN, D, FF, E = 8, 32, 4, 180, 768, 3072, 128
QT = QD * QL
PP = 192
ZX = 16
YC = 8
HALF = PD * PP
PT = PD * PLN
RB = PT // 3
DW = 768
CW = 512
CH = D // ZX
N_DEV = 128


def butterfly(x, lane):
    for k in (1, 2, 4, 8, 16):
        up = pltpu.roll(x, k, 1)
        down = pltpu.roll(x, 128 - k, 1)
        x = x + jnp.where((lane & k) != 0, up, down)
    return x


def kernel(
    qs, ps, qlen, plen, ids, pos, upw, upb, dnw, dnb, gain, bias, pw,
    loss_out, pg_out, gr_out,
    xq, xs, xb, wup, wdn, act, acc, hid, nrm, inv, qall, pall, ptr, axall, kpo, kpr, keepm,
    wts, tot, scr, onh, fac, msg, lmsg, sg, sgw, pgacc, qg, qr, psend, precv, gi, gradb, rs, mid, grb,
    ld_sem, up_sem, dn_sem, q_ss, q_rs, a_ss, a_rs, k_sem, p_sem, m_ss, m_rs, l_ss, l_rs,
    g_ss, g_rs, pg_sem, r_ss, r_rs, c_ss, c_rs, f_ss, f_rs, o_sem,
):
    rep, dp = lax.axis_index("rep"), lax.axis_index("dp")
    y, zx = lax.div(dp, ZX), lax.rem(dp, ZX)
    z, x = lax.div(zx, 4), lax.rem(zx, 4)
    other = lax.rem(dp + ZX, 2 * ZX)
    col = rep * 2 + y

    def member(k):
        return lax.rem(z + lax.div(k, 4), 4) * 4 + lax.rem(x + lax.rem(k, 4), 4)

    def source(k):
        return lax.rem(z + 4 - lax.div(k, 4), 4) * 4 + lax.rem(x + 4 - lax.rem(k, 4), 4)

    def row_dev(m):
        return (rep, y * ZX + m)

    def col_dev(m):
        return (lax.div(m, 2), lax.rem(m, 2) * ZX + zx)

    def remote(src, dst, ss, rs_, dev):
        return pltpu.make_async_remote_copy(
            src_ref=src, dst_ref=dst, send_sem=ss, recv_sem=rs_, device_id=dev, device_id_type=MESH
        )

    load_q = pltpu.make_async_copy(qs, xq, ld_sem.at[0])
    load_p = pltpu.make_async_copy(ps, xs, ld_sem.at[1])
    ups = [
        pltpu.make_async_copy(upw.at[:, pl.ds(c * DW, DW)], wup.at[:, pl.ds(c * DW, DW)], up_sem.at[c])
        for c in range(FF // DW)
    ]
    dns = [
        pltpu.make_async_copy(dnw.at[pl.ds(c * DW, DW)], wdn.at[pl.ds(c * DW, DW)], dn_sem.at[c])
        for c in range(FF // DW)
    ]
    load_q.start()
    for copy in ups + dns:
        copy.start()
    load_p.start()

    barrier = pltpu.get_barrier_semaphore()

    @pl.loop(1, ZX)
    def _(k):
        pl.semaphore_signal(barrier, inc=1, device_id=row_dev(member(k)), device_id_type=MESH)

    @pl.loop(1, YC)
    def _(k):
        pl.semaphore_signal(barrier, inc=1, device_id=col_dev(lax.rem(col + k, YC)), device_id_type=MESH)

    lane = lax.broadcasted_iota(jnp.int32, (8, 128), 1)
    row8 = lax.broadcasted_iota(jnp.int32, (8, 128), 0)
    for c in range(2):
        qn = lax.shift_right_logical(lane, 5) + 4 * c
        lens = jnp.zeros((8, 128), jnp.int32)
        posv = jnp.zeros((8, 128), jnp.int32)
        for n in range(4 * c, 4 * c + 4):
            lens = jnp.where(qn == n, qlen[n], lens)
            posv = jnp.where(qn == n, pos[n], posv)
        keep = ((lane & 31) < lens).astype(f32)
        axall[zx, c] = jnp.where(row8 == 0, keep, posv.astype(f32))
    kpo[...] = jnp.zeros(kpo.shape, f32)
    tcol = lax.broadcasted_iota(jnp.int32, (PD, PLN), 1)
    prow = lax.broadcasted_iota(jnp.int32, (PD, PLN), 0)
    plens = jnp.zeros((PD, PLN), jnp.int32)
    for k in range(PD):
        plens = jnp.where(prow == k, plen[k], plens)
    idv = ids[...]
    good = (tcol < plens) & ((idv < punct_low) | (idv >= punct_high))
    kpo[0:PD, 0:PLN] = good.astype(f32)
    pall[0:PD] = jnp.zeros((PD, PP, E), bf16)

    def encode(xv, rows, slot, wait_up, wait_down):
        for c in range(FF // CW):
            wait_up(c)
            cs = slice(c * CW, (c + 1) * CW)
            up = jnp.dot(xv(), wup[:, cs], preferred_element_type=f32) + upb[:, cs]
            act[slot, 0:rows, cs] = ((0.5 * up) * (1.0 + lax.erf(up * (1.0 / math.sqrt(2.0))))).astype(bf16)
        wait_down()
        down = jnp.dot(act[slot, 0:rows, :], wdn[...], preferred_element_type=f32)
        acc[slot, 0:rows, :] = down + (xv().astype(f32) + dnb[...].reshape(1, D))
        res = acc[slot, 0:rows, :]
        cen = res - jnp.mean(res, -1, keepdims=True)
        var = jnp.mean(cen * cen, -1, keepdims=True)
        scaled = cen * lax.rsqrt(var + eps_norm) * gain[...].reshape(1, D) + bias[...].reshape(1, D)
        h = scaled.astype(bf16)
        proj = jnp.dot(h, pw[...], preferred_element_type=f32)
        iv = lax.rsqrt(jnp.sum(proj * proj, -1, keepdims=True) + eps_norm)
        return h, proj * iv, jnp.broadcast_to(iv, proj.shape)

    load_q.wait()
    waited = set()

    def wait_up(c):
        for part in range((c * CW) // DW, ((c + 1) * CW - 1) // DW + 1):
            if part not in waited:
                waited.add(part)
                ups[part].wait()

    def wait_down():
        for copy in dns:
            copy.wait()

    h, n, iv = encode(lambda: xq[...], QT, 0, wait_up, wait_down)
    hid[0:QT, :] = h
    nrm[0:QT, :] = n
    inv[0:QT, :] = iv
    qall[zx] = n.astype(bf16)

    pl.semaphore_wait(barrier, ZX - 1 + YC - 1)

    def q_copy(slot, m):
        return remote(qall.at[slot], qall.at[slot], q_ss.at[m], q_rs.at[slot], row_dev(m))

    def a_copy(slot, m):
        return remote(axall.at[slot], axall.at[slot], a_ss.at[m], a_rs.at[slot], row_dev(m))

    @pl.loop(1, ZX)
    def _(k):
        m = member(k)
        q_copy(zx, m).start()
        a_copy(zx, m).start()

    k_copy = remote(kpo.at[pl.ds(0, 8)], kpr.at[pl.ds(0, 8)], k_sem.at[0], k_sem.at[1], (rep, other))
    k_copy.start()

    load_p.wait()
    xb[...] = xs[...].reshape(PT, D)
    for r in range(PT // RB):
        rows = slice(r * RB, (r + 1) * RB)
        h, n, iv = encode(lambda: xb[rows, :], RB, (r + 1) % 2, lambda c: None, lambda: None)
        at = slice(QT + r * RB, QT + (r + 1) * RB)
        hid[at, :] = h
        nrm[at, :] = n
        inv[at, :] = iv
    for k in range(PD):
        pall[k, 0:PLN, :] = nrm[pl.ds(QT + k, PLN, stride=PD), :].astype(bf16)

    p_copy = remote(pall.at[pl.ds(0, PD)], pall.at[pl.ds(PD, PD)], p_sem.at[0], p_sem.at[1], (rep, other))
    p_copy.start()

    def make_masks(src, base):
        v = jnp.transpose(src[...])
        for k in range(PD):
            keepm[base + k] = jnp.broadcast_to(v[0:PP, k : k + 1], (PP, 128))

    def make_ptr(h):
        v = pall[h * PD : (h + 1) * PD].reshape(HALF, E).astype(f32)
        ptr[:, h * HALF : (h + 1) * HALF] = jnp.transpose(v).astype(bf16)

    scale = math.log2(math.e) / temper

    def forward(j, h):
        q = qall[j]
        for k in range(PD):
            p = h * PD + k
            s = lax.dot_general(pall[p], q, (((1,), (1,)), ((), ())), preferred_element_type=f32)
            km = keepm[p]
            for c in range(2):
                w = jnp.exp2(s[:, c * 128 : (c + 1) * 128] * scale) * km
                wts[j, p * PP : (p + 1) * PP, c * 128 : (c + 1) * 128] = w
                tot[j, c, p : p + 1, :] = jnp.sum(w, axis=0, keepdims=True)

    make_masks(kpo, 0)
    make_ptr(0)

    @pl.loop(0, 4)
    def _(g):
        base = 4 * lax.rem(z + 4 - g, 4)
        for i in range(4):

            @pl.when(base + i != zx)
            def _():
                q_copy(base + i, base + i).wait_recv()
                a_copy(base + i, base + i).wait_recv()

        for i in range(4):
            forward(base + i, 0)

    k_copy.wait_recv()
    p_copy.wait_recv()
    make_masks(kpr, PD)
    make_ptr(1)

    @pl.loop(0, 4)
    def _(g):
        for i in range(4):
            forward(4 * g + i, 1)

    shape4 = (ZX, 2, 8, 128)
    flat = (ZX * 2 * 8, 128)
    lane2 = lax.broadcasted_iota(jnp.int32, flat, 1)
    soft = temper * jnp.log(tot[...]) * axall[:, :, 0:1, :]
    s4 = butterfly(soft.reshape(flat), lane2).reshape(shape4)
    pidx = lax.broadcasted_iota(jnp.int32, shape4, 2)
    pid = jnp.where(pidx < PD, dp * PD + pidx, other * PD + pidx - PD).astype(f32)
    one = (jnp.broadcast_to(axall[:, :, 1:2, :], shape4) == pid).astype(f32)
    pick = (lax.broadcasted_iota(jnp.int32, shape4, 3) & 31) == (
        lax.broadcasted_iota(jnp.int32, shape4, 0) * 2 + lax.broadcasted_iota(jnp.int32, shape4, 1)
    )
    se = jnp.sum(jnp.sum(jnp.where(pick, jnp.exp(s4), 0.0), axis=(0, 1)), axis=0, keepdims=True)
    po = jnp.sum(jnp.sum(jnp.where(pick, s4 * one, 0.0), axis=(0, 1)), axis=0, keepdims=True)
    msg[zx] = jnp.where(row8 == 0, se, jnp.where(row8 == 1, po, 0.0))
    scr[...] = s4
    onh[...] = one

    def m_copy(slot, m):
        return remote(msg.at[slot], msg.at[slot], m_ss.at[m], m_rs.at[slot], row_dev(m))

    @pl.loop(1, ZX)
    def _(k):
        m_copy(zx, member(k)).start()

    @pl.loop(1, ZX)
    def _(k):
        j = source(k)
        m_copy(j, j).wait_recv()

    both = jnp.sum(msg[...], axis=0)
    lt = jnp.log(both[0:1, :])
    lx = butterfly(
        jnp.where(pick, jnp.broadcast_to(lt.reshape(1, 1, 1, 128), shape4), 0.0).reshape(flat), lane2
    ).reshape(shape4)
    dsc = jnp.exp(scr[...] - lx) - onh[...]
    fac[...] = (dsc * axall[:, :, 0:1, :]) / tot[...]
    loss_row = jnp.sum(lt - both[1:2, :], axis=1, keepdims=True)
    lmsg[col] = jnp.broadcast_to(loss_row, (8, 128))

    def g_copy(src, dst, m):
        return remote(qg.at[src], qr.at[dst], g_ss.at[src], g_rs.at[dst], row_dev(m))

    def weighted(j, c, p):
        part = wts[j, p * PP : (p + 1) * PP, c * 128 : (c + 1) * 128]
        return (part * fac[j, c, p : p + 1, :]).astype(bf16)

    @pl.loop(0, 4)
    def _(g):
        base = 4 * lax.rem(z + 1 + g, 4)
        for i in range(4):
            for p in range(2 * PD):
                for c in range(2):
                    sg[i, p * PP : (p + 1) * PP, c * 128 : (c + 1) * 128] = weighted(base + i, c, p)
            qg[base + i] = jnp.dot(ptr[...], sg[i], preferred_element_type=f32).astype(bf16)
        for i in range(4):

            @pl.when(base + i != zx)
            def _():
                g_copy(base + i, zx, base + i).start()

    qr[zx] = qg[zx]

    def l_copy(slot, m):
        return remote(lmsg.at[slot], lmsg.at[slot], l_ss.at[m], l_rs.at[slot], col_dev(m))

    @pl.loop(1, YC)
    def _(k):
        l_copy(col, lax.rem(col + k, YC)).start()

    def passage_part(h):
        hs = slice(h * HALF, (h + 1) * HALF)

        @pl.loop(0, 4)
        def _(g):
            for k in range(PD):
                for i in range(4):
                    for c in range(2):
                        sgw[k * PP : (k + 1) * PP, i * QT + c * 128 : i * QT + (c + 1) * 128] = weighted(
                            4 * g + i, c, h * PD + k
                        )
            q4 = qall[pl.ds(4 * g, 4)].reshape(4 * QT, E)
            part = jnp.dot(sgw[...], q4, preferred_element_type=f32)

            @pl.when(g == 0)
            def _():
                pgacc[hs, :] = part

            @pl.when(g > 0)
            def _():
                pgacc[hs, :] += part

    passage_part(1)
    psend[...] = pgacc[HALF:, :].astype(bf16)
    pg_copy = remote(psend, precv, pg_sem.at[0], pg_sem.at[1], (rep, other))
    pg_copy.start()
    passage_part(0)

    pg_copy.wait_recv()

    def backward(g, at):
        n = nrm[at, :]
        return (inv[at, :] * (g - n * jnp.sum(n * g, -1, keepdims=True))).astype(bf16)

    def outer(b, at):
        return lax.dot_general(b, hid[at, :], (((0,), (0,)), ((), ())), preferred_element_type=f32)

    for k in range(PD):
        gi[pl.ds(k, PLN, stride=PD), :] = pgacc[k * PP : k * PP + PLN, :] + precv[
            k * PP : k * PP + PLN, :
        ].astype(f32)
    out_copy = pltpu.make_async_copy(gi, pg_out, o_sem)
    out_copy.start()
    prows, qrows = slice(QT, QT + PT), slice(0, QT)
    gt = outer(backward(gi[...], prows), prows)

    @pl.loop(1, ZX)
    def _(k):
        j = source(k)
        g_copy(j, j, j).wait_recv()

    qsum = jnp.sum(qr[...].astype(f32), axis=0)
    gt = gt + outer(backward(jnp.transpose(qsum), qrows), qrows)
    gradb[...] = jnp.transpose(gt).astype(bf16)

    def r_copy(src, dst, m):
        return remote(gradb.at[pl.ds(src * CH, CH)], rs.at[dst], r_ss.at[src], r_rs.at[dst], row_dev(m))

    @pl.loop(1, ZX)
    def _(k):
        m = member(k)
        r_copy(m, zx, m).start()

    mine = pl.ds(pl.multiple_of(zx * CH, 16), CH)
    rs[zx] = gradb[mine, :]

    @pl.loop(1, ZX)
    def _(k):
        j = source(k)
        r_copy(j, j, j).wait_recv()

    mid[col] = jnp.sum(rs[...].astype(f32), axis=0).astype(bf16)

    def c_copy(slot, m):
        return remote(mid.at[slot], mid.at[slot], c_ss.at[m], c_rs.at[slot], col_dev(m))

    @pl.loop(1, YC)
    def _(k):
        c_copy(col, lax.rem(col + k, YC)).start()

    @pl.loop(1, YC)
    def _(k):
        m = lax.rem(col + k, YC)
        c_copy(m, m).wait_recv()
        l_copy(m, m).wait_recv()

    grb[mine, :] = jnp.sum(mid[...].astype(f32), axis=0).astype(bf16)

    def f_copy(slot, m):
        rows = pl.ds(pl.multiple_of(slot * CH, 16), CH)
        return remote(grb.at[rows], grb.at[rows], f_ss.at[m], f_rs.at[slot], row_dev(m))

    @pl.loop(1, ZX)
    def _(k):
        f_copy(zx, member(k)).start()

    loss_out[...] = jnp.sum(lmsg[...], axis=0) * (1.0 / (N_DEV * QD))

    @pl.loop(1, ZX)
    def _(k):
        j = source(k)
        f_copy(j, j).wait_recv()

    gr_out[...] = grb[...].astype(f32)

    @pl.loop(1, ZX)
    def _(k):
        m = member(k)
        q_copy(zx, m).wait_send()
        a_copy(zx, m).wait_send()
        m_copy(zx, m).wait_send()
        g_copy(m, zx, m).wait_send()
        r_copy(m, zx, m).wait_send()
        f_copy(zx, m).wait_send()

    @pl.loop(1, YC)
    def _(k):
        c_copy(col, lax.rem(col + k, YC)).wait_send()
        l_copy(col, lax.rem(col + k, YC)).wait_send()

    k_copy.wait_send()
    p_copy.wait_send()
    pg_copy.wait_send()
    out_copy.wait()


def hand_out(loss, pgrad, grad, loss_out, pg_out, gr_out, pbuf, gbuf, sem):
    loads = [pltpu.make_async_copy(pgrad, pbuf, sem.at[0]), pltpu.make_async_copy(grad, gbuf, sem.at[1])]
    stores = [pltpu.make_async_copy(pbuf, pg_out, sem.at[2]), pltpu.make_async_copy(gbuf, gr_out, sem.at[3])]
    for copy in loads:
        copy.start()
    loss_out[...] = loss[0:1, 0:1]
    for load, store in zip(loads, stores):
        load.wait()
        store.start()
    for copy in stores:
        copy.wait()


def per_device(qs, ps, qlen, plen, ids, pos, upw, upb, dnw, dnb, gain, bias, pw):
    anyspace = pl.BlockSpec(memory_space=pl.ANY)
    vm = pl.BlockSpec(memory_space=pltpu.VMEM)
    sm = pl.BlockSpec(memory_space=pltpu.SMEM)
    dma = pltpu.SemaphoreType.DMA
    quad = pltpu.VMEM((ZX, 2, 8, 128), f32)
    outs = (
        jax.ShapeDtypeStruct((8, 128), f32),
        jax.ShapeDtypeStruct((PT, E), f32),
        jax.ShapeDtypeStruct((D, E), f32),
    )
    loss, pgrad, grad = pl.pallas_call(
        kernel,
        name="step",
        out_shape=outs,
        in_specs=[anyspace, anyspace, sm, sm, vm, sm, anyspace, vm, anyspace, vm, vm, vm, vm],
        out_specs=(vm, anyspace, vm),
        scratch_shapes=[
            pltpu.VMEM((QT, D), bf16),
            pltpu.VMEM((PLN, PD, D), bf16),
            pltpu.VMEM((PT, D), bf16),
            pltpu.VMEM((D, FF), bf16),
            pltpu.VMEM((FF, D), bf16),
            pltpu.VMEM((2, QT, FF), bf16),
            pltpu.VMEM((2, QT, D), f32),
            pltpu.VMEM((QT + PT, D), bf16),
            pltpu.VMEM((QT + PT, E), f32),
            pltpu.VMEM((QT + PT, E), f32),
            pltpu.VMEM((ZX, QT, E), bf16),
            pltpu.VMEM((2 * PD, PP, E), bf16),
            pltpu.VMEM((E, 2 * HALF), bf16),
            quad,
            pltpu.VMEM((128, 256), f32),
            pltpu.VMEM((128, 256), f32),
            pltpu.VMEM((2 * PD, PP, 128), f32),
            pltpu.VMEM((ZX, 2 * HALF, QT), f32),
            quad, quad, quad, quad,
            pltpu.VMEM((ZX, 8, 128), f32),
            pltpu.VMEM((YC, 8, 128), f32),
            pltpu.VMEM((4, 2 * HALF, QT), bf16),
            pltpu.VMEM((HALF, 4 * QT), bf16),
            pltpu.VMEM((2 * HALF, E), f32),
            pltpu.VMEM((ZX, E, QT), bf16),
            pltpu.VMEM((ZX, E, QT), bf16),
            pltpu.VMEM((HALF, E), bf16),
            pltpu.VMEM((HALF, E), bf16),
            pltpu.VMEM((PT, E), f32),
            pltpu.VMEM((D, E), bf16),
            pltpu.VMEM((ZX, CH, E), bf16),
            pltpu.VMEM((YC, CH, E), bf16),
            pltpu.VMEM((D, E), bf16),
            dma((2,)), dma((4,)), dma((4,)),
            dma((ZX,)), dma((ZX,)), dma((ZX,)), dma((ZX,)),
            dma((2,)), dma((2,)), dma((ZX,)), dma((ZX,)), dma((YC,)), dma((YC,)),
            dma((ZX,)), dma((ZX,)), dma((2,)), dma((ZX,)), dma((ZX,)),
            dma((YC,)), dma((YC,)), dma((ZX,)), dma((ZX,)), dma,
        ],
        compiler_params=pltpu.CompilerParams(
            collective_id=0, has_side_effects=True, vmem_limit_bytes=62 * 1024 * 1024
        ),
    )(
        qs.reshape(QT, D), ps.transpose(1, 0, 2), qlen, plen, ids, pos,
        upw, upb.reshape(1, FF), dnw, dnb, gain, bias, pw,
    )
    loss, pgrad, grad = pl.pallas_call(
        hand_out,
        name="hand_out",
        out_shape=(jax.ShapeDtypeStruct((1, 1), f32), *outs[1:]),
        in_specs=[vm, anyspace, anyspace],
        out_specs=(vm, anyspace, anyspace),
        scratch_shapes=[pltpu.VMEM((PT, E), f32), pltpu.VMEM((D, E), f32), dma((4,))],
    )(loss, pgrad, grad)
    return loss.reshape(()), pgrad.reshape(PLN, PD, E).transpose(1, 0, 2), grad


def solution(mesh):
    both = ("rep", "dp")
    in_specs = (
        P(both, None, None), P(both, None, None), P(both), P(both), P(both, None), P(both),
        P(), P(), P(), P(), P(), P(), P(),
    )
    out_specs = (P(), P(both, None, None), P())
    return jax.shard_map(per_device, mesh=mesh, in_specs=in_specs, out_specs=out_specs, check_vma=False)
```

time: 95.3 us -> 77.9 us (0.82)
  local copies, waits for them, and re-layouts: 10.9 us -> 0 us
  Pallas kernels: 83.4 us -> 76.9 us
    pallas_call x1 -> x2, Pallas kernels: 83.4 us -> 76.9 us  [the longest x1 73.8 us: per_device(): pl.pallas_call(kernel, name='step', out_shape=outs, in_specs=[anyspace, a...]
    unnamed x3 -> x0, local copies, waits for them, and re-layouts: 5.95 us -> none
    reshape x3 -> x0, local copies, waits for them, and re-layouts: 3.8 us -> none  [the longest x1 1.27 us: per_device(): dnb.reshape(1, D)]
    slice x1 -> x0, local copies, waits for them, and re-layouts: 1.19 us -> none  [per_device(): return (loss[0, 0], pgrad, grad)]
where the time goes in v2:
time: 77.9 us; the launch traced here: 77.7 us
  Pallas kernels  76.9 us (99%)
  between operations  0.8 us (1%)
    pallas_call x1, Pallas kernels, per_device(): pl.pallas_call(kernel, name='step', out_shape=outs, in_specs=[anyspace, a...  73.8 us
    pallas_call x1, Pallas kernels, per_device(): pl.pallas_call(hand_out, name='hand_out', out_shape=(jax.ShapeDtypeStruct...  3.07 us

profile of v2, /device:TPU:0, one launch (start us, length us, event | category | flops | bytes accessed | tf_op | source)
XLA Modules:
  0.0 77.7 jit_solution(6377865036668759448)
XLA Ops:
  0.6 73.8 %step.1 = (f32[8,128]{1,0:T(8,128)}, f32[720,128]{1,0:T(8,128)}, f32[768,128]{1,0:T(8,128)}) custom-call(bf16[256,768]{1,0:T(8,128)(2,1)} %bitcast.8, bf16[180,4,768]{2,1,0:T(4,128)(2,1)} %bitcast.7, s32[8]{0:T(128)} %qlen.1, s32[4]{0:T(128)} %plen.1, s32[4,180]{1,0:T(4,128)} %ids.1, s32[8]{0:T(128)} %pos.1, bf16[768,3072]{1,0:T(8,128)(2,1)} %upw.1, ...), custom_call_target="tpu_custom_call" | custom-call | tf_op jit(solution)/shard_map/step/pallas_call | solution.py:455
  74.5 3.1 %hand_out.1 = (f32[1,1]{1,0:T(1,128)}, f32[720,128]{1,0:T(8,128)}, f32[768,128]{1,0:T(8,128)}) custom-call(f32[8,128]{1,0:T(8,128)} %get-tuple-element.9.loss, f32[720,128]{1,0:T(8,128)} %get-tuple-element.10.pgrad, f32[768,128]{1,0:T(8,128)} %get-tuple-element.11.grad), custom_call_target="tpu_custom_call" | custom-call | tf_op jit(solution)/shard_map/hand_out/pallas_call | solution.py:508

commit v3 on v2

--- a/solution.py
+++ b/solution.py
@@ -24,7 +24,7 @@
 HALF = PD * PP
 PT = PD * PLN
 RB = PT // 3
-DW = 768
+DW = 1536
 CW = 512
 CH = D // ZX
 N_DEV = 128
@@ -39,12 +39,12 @@
 
 
 def kernel(
-    qs, ps, qlen, plen, ids, pos, upw, upb, dnw, dnb, gain, bias, pw,
-    loss_out, pg_out, gr_out,
-    xq, xs, xb, wup, wdn, act, acc, hid, nrm, inv, qall, pall, ptr, axall, kpo, kpr, keepm,
-    wts, tot, scr, onh, fac, msg, lmsg, sg, sgw, pgacc, qg, qr, psend, precv, gi, gradb, rs, mid, grb,
+    qs, ps, qlen_in, plen_in, ids_in, pos_in, upw, upb_in, dnw, dnb_in, gain_in, bias_in, pw_in,
+    loss_out, gi, gr_out,
+    qlen, plen, pos, ids, upb, dnb, gain, bias, pw, xq, xs, xb, wup, wdn, act, acc, hid, nrm, inv, qall, pall, ptr, axall, kpo, kpr, keepm,
+    wts, tot, scr, onh, fac, msg, lmsg, sg, sgw, pgacc, qg, qr, psend, precv, gradb, rs, mid, grb,
     ld_sem, up_sem, dn_sem, q_ss, q_rs, a_ss, a_rs, k_sem, p_sem, m_ss, m_rs, l_ss, l_rs,
-    g_ss, g_rs, pg_sem, r_ss, r_rs, c_ss, c_rs, f_ss, f_rs, o_sem,
+    g_ss, g_rs, pg_sem, r_ss, r_rs, c_ss, c_rs, f_ss, f_rs, s_sem,
 ):
     rep, dp = lax.axis_index("rep"), lax.axis_index("dp")
     y, zx = lax.div(dp, ZX), lax.rem(dp, ZX)
@@ -55,14 +55,14 @@
     def member(k):
         return lax.rem(z + lax.div(k, 4), 4) * 4 + lax.rem(x + lax.rem(k, 4), 4)
 
-    def source(k):
-        return lax.rem(z + 4 - lax.div(k, 4), 4) * 4 + lax.rem(x + 4 - lax.rem(k, 4), 4)
-
     def row_dev(m):
         return (rep, y * ZX + m)
 
     def col_dev(m):
         return (lax.div(m, 2), lax.rem(m, 2) * ZX + zx)
+
+    def several(ref, n, ss, rs_):
+        return remote(ref.at[pl.ds(0, n)], ref.at[pl.ds(0, n)], ss, rs_, (rep, other))
 
     def remote(src, dst, ss, rs_, dev):
         return pltpu.make_async_remote_copy(
@@ -79,8 +79,21 @@
         pltpu.make_async_copy(dnw.at[pl.ds(c * DW, DW)], wdn.at[pl.ds(c * DW, DW)], dn_sem.at[c])
         for c in range(FF // DW)
     ]
+    small = [
+        pltpu.make_async_copy(a, b, s_sem.at[i])
+        for i, (a, b) in enumerate(
+            (
+                (qlen_in, qlen), (plen_in, plen), (pos_in, pos), (ids_in, ids), (upb_in, upb),
+                (dnb_in, dnb), (gain_in, gain), (bias_in, bias), (pw_in, pw),
+            )
+        )
+    ]
+    for copy in small[:4]:
+        copy.start()
     load_q.start()
-    for copy in ups + dns:
+    ups[0].start()
+    small[4].start()
+    for copy in ups[1:] + small[5:] + dns:
         copy.start()
     load_p.start()
 
@@ -94,6 +107,10 @@
     def _(k):
         pl.semaphore_signal(barrier, inc=1, device_id=col_dev(lax.rem(col + k, YC)), device_id_type=MESH)
 
+    pall[0:PD] = jnp.zeros((PD, PP, E), bf16)
+    kpo[...] = jnp.zeros(kpo.shape, f32)
+    for copy in small[:4]:
+        copy.wait()
     lane = lax.broadcasted_iota(jnp.int32, (8, 128), 1)
     row8 = lax.broadcasted_iota(jnp.int32, (8, 128), 0)
     for c in range(2):
@@ -105,7 +122,6 @@
             posv = jnp.where(qn == n, pos[n], posv)
         keep = ((lane & 31) < lens).astype(f32)
         axall[zx, c] = jnp.where(row8 == 0, keep, posv.astype(f32))
-    kpo[...] = jnp.zeros(kpo.shape, f32)
     tcol = lax.broadcasted_iota(jnp.int32, (PD, PLN), 1)
     prow = lax.broadcasted_iota(jnp.int32, (PD, PLN), 0)
     plens = jnp.zeros((PD, PLN), jnp.int32)
@@ -114,7 +130,24 @@
     idv = ids[...]
     good = (tcol < plens) & ((idv < punct_low) | (idv >= punct_high))
     kpo[0:PD, 0:PLN] = good.astype(f32)
-    pall[0:PD] = jnp.zeros((PD, PP, E), bf16)
+
+    pl.semaphore_wait(barrier, ZX - 1 + YC - 1)
+    far_first = sorted(range(1, ZX), key=lambda k: -(min(k // 4, 4 - k // 4) + min(k % 4, 4 - k % 4)))
+
+    def a_copy(slot, m):
+        return remote(axall.at[slot], axall.at[slot], a_ss, a_rs, row_dev(m))
+
+    for k in far_first:
+        a_copy(zx, member(k)).start()
+    k_copy = remote(kpo.at[pl.ds(0, 8)], kpr.at[pl.ds(0, 8)], k_sem.at[0], k_sem.at[1], (rep, other))
+    k_copy.start()
+
+    def make_masks(src, base):
+        v = jnp.transpose(src[...])
+        for k in range(PD):
+            keepm[base + k] = jnp.broadcast_to(v[0:PP, k : k + 1], (PP, 128))
+
+    make_masks(kpo, 0)
 
     def encode(xv, rows, slot, wait_up, wait_down):
         for c in range(FF // CW):
@@ -122,9 +155,17 @@
             cs = slice(c * CW, (c + 1) * CW)
             up = jnp.dot(xv(), wup[:, cs], preferred_element_type=f32) + upb[:, cs]
             act[slot, 0:rows, cs] = ((0.5 * up) * (1.0 + lax.erf(up * (1.0 / math.sqrt(2.0))))).astype(bf16)
-        wait_down()
-        down = jnp.dot(act[slot, 0:rows, :], wdn[...], preferred_element_type=f32)
-        acc[slot, 0:rows, :] = down + (xv().astype(f32) + dnb[...].reshape(1, D))
+        if wait_down is None:
+            down = jnp.dot(act[slot, 0:rows, :], wdn[...], preferred_element_type=f32)
+            acc[slot, 0:rows, :] = down + (xv().astype(f32) + dnb[...].reshape(1, D))
+        else:
+            for copy in small[5:]:
+                copy.wait()
+            acc[slot, 0:rows, :] = xv().astype(f32) + dnb[...].reshape(1, D)
+            for c in range(FF // DW):
+                wait_down(c)
+                cs = slice(c * DW, (c + 1) * DW)
+                acc[slot, 0:rows, :] += jnp.dot(act[slot, 0:rows, cs], wdn[cs, :], preferred_element_type=f32)
         res = acc[slot, 0:rows, :]
         cen = res - jnp.mean(res, -1, keepdims=True)
         var = jnp.mean(cen * cen, -1, keepdims=True)
@@ -135,6 +176,7 @@
         return h, proj * iv, jnp.broadcast_to(iv, proj.shape)
 
     load_q.wait()
+    small[4].wait()
     waited = set()
 
     def wait_up(c):
@@ -143,38 +185,23 @@
                 waited.add(part)
                 ups[part].wait()
 
-    def wait_down():
-        for copy in dns:
-            copy.wait()
-
-    h, n, iv = encode(lambda: xq[...], QT, 0, wait_up, wait_down)
+    h, n, iv = encode(lambda: xq[...], QT, 0, wait_up, lambda c: dns[c].wait())
     hid[0:QT, :] = h
     nrm[0:QT, :] = n
     inv[0:QT, :] = iv
     qall[zx] = n.astype(bf16)
 
-    pl.semaphore_wait(barrier, ZX - 1 + YC - 1)
-
     def q_copy(slot, m):
-        return remote(qall.at[slot], qall.at[slot], q_ss.at[m], q_rs.at[slot], row_dev(m))
-
-    def a_copy(slot, m):
-        return remote(axall.at[slot], axall.at[slot], a_ss.at[m], a_rs.at[slot], row_dev(m))
-
-    @pl.loop(1, ZX)
-    def _(k):
-        m = member(k)
-        q_copy(zx, m).start()
-        a_copy(zx, m).start()
-
-    k_copy = remote(kpo.at[pl.ds(0, 8)], kpr.at[pl.ds(0, 8)], k_sem.at[0], k_sem.at[1], (rep, other))
-    k_copy.start()
+        return remote(qall.at[slot], qall.at[slot], q_ss, q_rs.at[lax.div(slot, 4)], row_dev(m))
+
+    for k in far_first:
+        q_copy(zx, member(k)).start()
 
     load_p.wait()
     xb[...] = xs[...].reshape(PT, D)
     for r in range(PT // RB):
         rows = slice(r * RB, (r + 1) * RB)
-        h, n, iv = encode(lambda: xb[rows, :], RB, (r + 1) % 2, lambda c: None, lambda: None)
+        h, n, iv = encode(lambda: xb[rows, :], RB, (r + 1) % 2, lambda c: None, None)
         at = slice(QT + r * RB, QT + (r + 1) * RB)
         hid[at, :] = h
         nrm[at, :] = n
@@ -184,11 +211,6 @@
 
     p_copy = remote(pall.at[pl.ds(0, PD)], pall.at[pl.ds(PD, PD)], p_sem.at[0], p_sem.at[1], (rep, other))
     p_copy.start()
-
-    def make_masks(src, base):
-        v = jnp.transpose(src[...])
-        for k in range(PD):
-            keepm[base + k] = jnp.broadcast_to(v[0:PP, k : k + 1], (PP, 128))
 
     def make_ptr(h):
         v = pall[h * PD : (h + 1) * PD].reshape(HALF, E).astype(f32)
@@ -207,24 +229,27 @@
                 wts[j, p * PP : (p + 1) * PP, c * 128 : (c + 1) * 128] = w
                 tot[j, c, p : p + 1, :] = jnp.sum(w, axis=0, keepdims=True)
 
-    make_masks(kpo, 0)
     make_ptr(0)
 
     @pl.loop(0, 4)
     def _(g):
-        base = 4 * lax.rem(z + 4 - g, 4)
-        for i in range(4):
-
-            @pl.when(base + i != zx)
-            def _():
-                q_copy(base + i, base + i).wait_recv()
-                a_copy(base + i, base + i).wait_recv()
+        row = lax.rem(z + 4 - g, 4)
+        base = 4 * row
+
+        @pl.when(g == 0)
+        def _():
+            several(qall, 3, q_ss, q_rs.at[row]).wait_recv()
+
+        @pl.when(g > 0)
+        def _():
+            several(qall, 4, q_ss, q_rs.at[row]).wait_recv()
 
         for i in range(4):
             forward(base + i, 0)
 
     k_copy.wait_recv()
     p_copy.wait_recv()
+    several(axall, ZX - 1, a_ss, a_rs).wait_recv()
     make_masks(kpr, PD)
     make_ptr(1)
 
@@ -251,16 +276,12 @@
     onh[...] = one
 
     def m_copy(slot, m):
-        return remote(msg.at[slot], msg.at[slot], m_ss.at[m], m_rs.at[slot], row_dev(m))
-
-    @pl.loop(1, ZX)
-    def _(k):
+        return remote(msg.at[slot], msg.at[slot], m_ss, m_rs, row_dev(m))
+
+    for k in far_first:
         m_copy(zx, member(k)).start()
 
-    @pl.loop(1, ZX)
-    def _(k):
-        j = source(k)
-        m_copy(j, j).wait_recv()
+    several(msg, ZX - 1, m_ss, m_rs).wait_recv()
 
     both = jnp.sum(msg[...], axis=0)
     lt = jnp.log(both[0:1, :])
@@ -273,30 +294,34 @@
     lmsg[col] = jnp.broadcast_to(loss_row, (8, 128))
 
     def g_copy(src, dst, m):
-        return remote(qg.at[src], qr.at[dst], g_ss.at[src], g_rs.at[dst], row_dev(m))
+        return remote(qg.at[src], qr.at[dst], g_ss, g_rs, row_dev(m))
 
     def weighted(j, c, p):
         part = wts[j, p * PP : (p + 1) * PP, c * 128 : (c + 1) * 128]
         return (part * fac[j, c, p : p + 1, :]).astype(bf16)
 
-    @pl.loop(0, 4)
+    def query_part(j, i):
+        for p in range(2 * PD):
+            for c in range(2):
+                sg[i, p * PP : (p + 1) * PP, c * 128 : (c + 1) * 128] = weighted(j, c, p)
+        return jnp.dot(ptr[...], sg[i], preferred_element_type=f32).astype(bf16)
+
+    @pl.loop(0, 3)
     def _(g):
-        base = 4 * lax.rem(z + 1 + g, 4)
+        row = 4 * lax.rem(z + 1 + lax.rem(g + 1, 3), 4)
         for i in range(4):
-            for p in range(2 * PD):
-                for c in range(2):
-                    sg[i, p * PP : (p + 1) * PP, c * 128 : (c + 1) * 128] = weighted(base + i, c, p)
-            qg[base + i] = jnp.dot(ptr[...], sg[i], preferred_element_type=f32).astype(bf16)
-        for i in range(4):
-
-            @pl.when(base + i != zx)
-            def _():
-                g_copy(base + i, zx, base + i).start()
-
-    qr[zx] = qg[zx]
+            j = row + lax.rem(x + 2 + i, 4)
+            qg[j] = query_part(j, i)
+            g_copy(j, zx, j).start()
+
+    for i, dx in enumerate((2, 1, 3)):
+        j = 4 * z + lax.rem(x + dx, 4)
+        qg[j] = query_part(j, i)
+        g_copy(j, zx, j).start()
+    qr[zx] = query_part(zx, 3)
 
     def l_copy(slot, m):
-        return remote(lmsg.at[slot], lmsg.at[slot], l_ss.at[m], l_rs.at[slot], col_dev(m))
+        return remote(lmsg.at[slot], lmsg.at[slot], l_ss, l_rs, col_dev(m))
 
     @pl.loop(1, YC)
     def _(k):
@@ -343,100 +368,73 @@
         gi[pl.ds(k, PLN, stride=PD), :] = pgacc[k * PP : k * PP + PLN, :] + precv[
             k * PP : k * PP + PLN, :
         ].astype(f32)
-    out_copy = pltpu.make_async_copy(gi, pg_out, o_sem)
-    out_copy.start()
     prows, qrows = slice(QT, QT + PT), slice(0, QT)
     gt = outer(backward(gi[...], prows), prows)
 
-    @pl.loop(1, ZX)
-    def _(k):
-        j = source(k)
-        g_copy(j, j, j).wait_recv()
+    several(qr, ZX - 1, g_ss, g_rs).wait_recv()
 
     qsum = jnp.sum(qr[...].astype(f32), axis=0)
     gt = gt + outer(backward(jnp.transpose(qsum), qrows), qrows)
     gradb[...] = jnp.transpose(gt).astype(bf16)
 
     def r_copy(src, dst, m):
-        return remote(gradb.at[pl.ds(src * CH, CH)], rs.at[dst], r_ss.at[src], r_rs.at[dst], row_dev(m))
-
-    @pl.loop(1, ZX)
-    def _(k):
+        return remote(gradb.at[pl.ds(pl.multiple_of(src * CH, 16), CH)], rs.at[dst], r_ss, r_rs, row_dev(m))
+
+    for k in far_first:
         m = member(k)
         r_copy(m, zx, m).start()
 
     mine = pl.ds(pl.multiple_of(zx * CH, 16), CH)
     rs[zx] = gradb[mine, :]
 
-    @pl.loop(1, ZX)
-    def _(k):
-        j = source(k)
-        r_copy(j, j, j).wait_recv()
+    several(rs, ZX - 1, r_ss, r_rs).wait_recv()
 
     mid[col] = jnp.sum(rs[...].astype(f32), axis=0).astype(bf16)
 
     def c_copy(slot, m):
-        return remote(mid.at[slot], mid.at[slot], c_ss.at[m], c_rs.at[slot], col_dev(m))
+        return remote(mid.at[slot], mid.at[slot], c_ss, c_rs, col_dev(m))
 
     @pl.loop(1, YC)
     def _(k):
         c_copy(col, lax.rem(col + k, YC)).start()
 
-    @pl.loop(1, YC)
-    def _(k):
-        m = lax.rem(col + k, YC)
-        c_copy(m, m).wait_recv()
-        l_copy(m, m).wait_recv()
+    several(mid, YC - 1, c_ss, c_rs).wait_recv()
 
     grb[mine, :] = jnp.sum(mid[...].astype(f32), axis=0).astype(bf16)
 
     def f_copy(slot, m):
         rows = pl.ds(pl.multiple_of(slot * CH, 16), CH)
-        return remote(grb.at[rows], grb.at[rows], f_ss.at[m], f_rs.at[slot], row_dev(m))
-
-    @pl.loop(1, ZX)
-    def _(k):
+        return remote(grb.at[rows], grb.at[rows], f_ss, f_rs, row_dev(m))
+
+    for k in far_first:
         f_copy(zx, member(k)).start()
 
-    loss_out[...] = jnp.sum(lmsg[...], axis=0) * (1.0 / (N_DEV * QD))
-
-    @pl.loop(1, ZX)
-    def _(k):
-        j = source(k)
-        f_copy(j, j).wait_recv()
+    several(lmsg, YC - 1, l_ss, l_rs).wait_recv()
+    loss_out[...] = jnp.sum(lmsg[...], axis=0)[0:1, 0:1] * (1.0 / (N_DEV * QD))
+
+    rest = (ZX - 1) * CH
+    several(grb, rest, f_ss, f_rs).wait_recv()
 
     gr_out[...] = grb[...].astype(f32)
 
-    @pl.loop(1, ZX)
-    def _(k):
-        m = member(k)
-        q_copy(zx, m).wait_send()
-        a_copy(zx, m).wait_send()
-        m_copy(zx, m).wait_send()
-        g_copy(m, zx, m).wait_send()
-        r_copy(m, zx, m).wait_send()
-        f_copy(zx, m).wait_send()
-
-    @pl.loop(1, YC)
-    def _(k):
-        c_copy(col, lax.rem(col + k, YC)).wait_send()
-        l_copy(col, lax.rem(col + k, YC)).wait_send()
-
+    several(qall, ZX - 1, q_ss, q_rs.at[0]).wait_send()
+    several(axall, ZX - 1, a_ss, a_rs).wait_send()
+    several(msg, ZX - 1, m_ss, m_rs).wait_send()
+    several(qg, ZX - 1, g_ss, g_rs).wait_send()
+    several(rs, ZX - 1, r_ss, r_rs).wait_send()
+    several(grb, rest, f_ss, f_rs).wait_send()
+    several(mid, YC - 1, c_ss, c_rs).wait_send()
+    several(lmsg, YC - 1, l_ss, l_rs).wait_send()
     k_copy.wait_send()
     p_copy.wait_send()
     pg_copy.wait_send()
-    out_copy.wait()
-
-
-def hand_out(loss, pgrad, grad, loss_out, pg_out, gr_out, pbuf, gbuf, sem):
-    loads = [pltpu.make_async_copy(pgrad, pbuf, sem.at[0]), pltpu.make_async_copy(grad, gbuf, sem.at[1])]
-    stores = [pltpu.make_async_copy(pbuf, pg_out, sem.at[2]), pltpu.make_async_copy(gbuf, gr_out, sem.at[3])]
-    for copy in loads:
+
+
+def hand_out(loss, pgrad, grad, loss_out, pg_out, gr_out, sem):
+    stores = [pltpu.make_async_copy(pgrad, pg_out, sem.at[0]), pltpu.make_async_copy(grad, gr_out, sem.at[1])]
+    for copy in stores:
         copy.start()
-    loss_out[...] = loss[0:1, 0:1]
-    for load, store in zip(loads, stores):
-        load.wait()
-        store.start()
+    loss_out[...] = loss[...]
     for copy in stores:
         copy.wait()
 
@@ -444,21 +442,29 @@
 def per_device(qs, ps, qlen, plen, ids, pos, upw, upb, dnw, dnb, gain, bias, pw):
     anyspace = pl.BlockSpec(memory_space=pl.ANY)
     vm = pl.BlockSpec(memory_space=pltpu.VMEM)
-    sm = pl.BlockSpec(memory_space=pltpu.SMEM)
     dma = pltpu.SemaphoreType.DMA
     quad = pltpu.VMEM((ZX, 2, 8, 128), f32)
     outs = (
-        jax.ShapeDtypeStruct((8, 128), f32),
+        jax.ShapeDtypeStruct((1, 1), f32),
         jax.ShapeDtypeStruct((PT, E), f32),
         jax.ShapeDtypeStruct((D, E), f32),
     )
     loss, pgrad, grad = pl.pallas_call(
         kernel,
         name="step",
-        out_shape=outs,
-        in_specs=[anyspace, anyspace, sm, sm, vm, sm, anyspace, vm, anyspace, vm, vm, vm, vm],
-        out_specs=(vm, anyspace, vm),
+        out_shape=tuple(pltpu.VMEM(o.shape, o.dtype) for o in outs),
+        in_specs=[anyspace] * 13,
+        out_specs=(vm, vm, vm),
         scratch_shapes=[
+            pltpu.SMEM((QD,), jnp.int32),
+            pltpu.SMEM((PD,), jnp.int32),
+            pltpu.SMEM((QD,), jnp.int32),
+            pltpu.VMEM((PD, PLN), jnp.int32),
+            pltpu.VMEM((1, FF), f32),
+            pltpu.VMEM((D,), f32),
+            pltpu.VMEM((D,), f32),
+            pltpu.VMEM((D,), f32),
+            pltpu.VMEM((D, E), bf16),
             pltpu.VMEM((QT, D), bf16),
             pltpu.VMEM((PLN, PD, D), bf16),
             pltpu.VMEM((PT, D), bf16),
@@ -487,16 +493,13 @@
             pltpu.VMEM((ZX, E, QT), bf16),
             pltpu.VMEM((HALF, E), bf16),
             pltpu.VMEM((HALF, E), bf16),
-            pltpu.VMEM((PT, E), f32),
             pltpu.VMEM((D, E), bf16),
             pltpu.VMEM((ZX, CH, E), bf16),
             pltpu.VMEM((YC, CH, E), bf16),
             pltpu.VMEM((D, E), bf16),
-            dma((2,)), dma((4,)), dma((4,)),
-            dma((ZX,)), dma((ZX,)), dma((ZX,)), dma((ZX,)),
-            dma((2,)), dma((2,)), dma((ZX,)), dma((ZX,)), dma((YC,)), dma((YC,)),
-            dma((ZX,)), dma((ZX,)), dma((2,)), dma((ZX,)), dma((ZX,)),
-            dma((YC,)), dma((YC,)), dma((ZX,)), dma((ZX,)), dma,
+            dma((2,)), dma((2,)), dma((2,)),
+            dma, dma((4,)), dma, dma, dma((2,)), dma((2,)), dma, dma, dma, dma,
+            dma, dma, dma((2,)), dma, dma, dma, dma, dma, dma, dma((9,)),
         ],
         compiler_params=pltpu.CompilerParams(
             collective_id=0, has_side_effects=True, vmem_limit_bytes=62 * 1024 * 1024
@@ -508,11 +511,11 @@
     loss, pgrad, grad = pl.pallas_call(
         hand_out,
         name="hand_out",
-        out_shape=(jax.ShapeDtypeStruct((1, 1), f32), *outs[1:]),
-        in_specs=[vm, anyspace, anyspace],
+        out_shape=outs,
+        in_specs=[vm, vm, vm],
         out_specs=(vm, anyspace, anyspace),
-        scratch_shapes=[pltpu.VMEM((PT, E), f32), pltpu.VMEM((D, E), f32), dma((4,))],
-    )(loss, pgrad, grad)
+        scratch_shapes=[dma((2,))],
+    )(*(pltpu.with_memory_space_constraint(a, pltpu.VMEM) for a in (loss, pgrad, grad)))
     return loss.reshape(()), pgrad.reshape(PLN, PD, E).transpose(1, 0, 2), grad
 
 

time: 77.9 us -> 70.7 us (0.908)
  Pallas kernels: 76.9 us -> 69.8 us
    pallas_call x2, Pallas kernels: 76.9 us -> 69.8 us  [the longest x1 67.8 us: per_device(): pl.pallas_call(kernel, name='step', out_shape=tuple((pltpu.VMEM(o.shape,...]
where the time goes in v3:
time: 70.7 us; the launch traced here: 70.6 us
  Pallas kernels  69.8 us (99%)
  between operations  0.8 us (1%)
    pallas_call x1, Pallas kernels, per_device(): pl.pallas_call(kernel, name='step', out_shape=tuple((pltpu.VMEM(o.shape,...  67.8 us
    pallas_call x1, Pallas kernels, per_device(): pl.pallas_call(hand_out, name='hand_out', out_shape=outs, in_specs=[vm, v...  2.03 us

profile of v3, /device:TPU:0, one launch (start us, length us, event | category | flops | bytes accessed | tf_op | source)
XLA Modules:
  0.0 70.6 jit_solution(2537416934143524227)
XLA Ops:
  0.6 67.8 %step.1 = (f32[1,1]{1,0:T(1,128)}, f32[720,128]{1,0:T(8,128)S(1)}, f32[768,128]{1,0:T(8,128)S(1)}) custom-call(bf16[256,768]{1,0:T(8,128)(2,1)} %bitcast.8, bf16[180,4,768]{2,1,0:T(4,128)(2,1)} %bitcast.7, s32[8]{0:T(128)} %qlen_in.1, s32[4]{0:T(128)} %plen_in.1, s32[4,180]{1,0:T(4,128)} %ids_in.1, s32[8]{0:T(128)} %pos_in.1, bf16[768,3072]{1,0:T(8,128)(2,1)} %upw.1, ...), custom_call_target="tpu_custom_call" | custom-call | tf_op jit(solution)/shard_map/step/pallas_call | solution.py:452
  68.4 2.0 %hand_out.1 = (f32[1,1]{1,0:T(1,128)}, f32[720,128]{1,0:T(8,128)}, f32[768,128]{1,0:T(8,128)}) custom-call(f32[1,1]{1,0:T(1,128)} %get-tuple-element.9.loss, f32[720,128]{1,0:T(8,128)S(1)} %get-tuple-element.10.pgrad, f32[768,128]{1,0:T(8,128)S(1)} %get-tuple-element.11.grad), custom_call_target="tpu_custom_call" | custom-call | tf_op jit(solution)/shard_map/hand_out/pallas_call | solution.py:511

commit v4 on v3

--- a/solution.py
+++ b/solution.py
@@ -23,7 +23,7 @@
 YC = 8
 HALF = PD * PP
 PT = PD * PLN
-RB = PT // 3
+TS = 64
 DW = 1536
 CW = 512
 CH = D // ZX
@@ -189,28 +189,51 @@
     hid[0:QT, :] = h
     nrm[0:QT, :] = n
     inv[0:QT, :] = iv
-    qall[zx] = n.astype(bf16)
-
-    def q_copy(slot, m):
-        return remote(qall.at[slot], qall.at[slot], q_ss, q_rs.at[lax.div(slot, 4)], row_dev(m))
-
-    for k in far_first:
-        q_copy(zx, member(k)).start()
+    qall[z, x] = n.astype(bf16)
+
+    low, high = pl.ds(0, QT // 2), pl.ds(QT // 2, QT // 2)
+
+    def at_z(d):
+        return (rep, y * ZX + lax.rem(z + d, 4) * 4 + x)
+
+    def at_x(d):
+        return (rep, y * ZX + z * 4 + lax.rem(x + d, 4))
+
+    def q_copy(block, stage, dev):
+        return remote(block, block, q_ss, q_rs.at[stage], dev)
+
+    for d in (2, 1, 3):
+        q_copy(qall.at[z, x, low], 0, at_z(d)).start()
+        q_copy(qall.at[z, x, high], 0, at_x(d)).start()
 
     load_p.wait()
     xb[...] = xs[...].reshape(PT, D)
-    for r in range(PT // RB):
-        rows = slice(r * RB, (r + 1) * RB)
-        h, n, iv = encode(lambda: xb[rows, :], RB, (r + 1) % 2, lambda c: None, None)
-        at = slice(QT + r * RB, QT + (r + 1) * RB)
+    def p_copy(r):
+        slots = pl.ds(r * TS, TS)
+        return remote(
+            pall.at[pl.ds(0, PD), slots], pall.at[pl.ds(PD, PD), slots], p_sem.at[0], p_sem.at[1], (rep, other)
+        )
+
+    for r in range(PP // TS):
+        slots = min(TS, PLN - r * TS)
+        first = r * TS * PD
+        rows = slice(first, first + slots * PD)
+        h, n, iv = encode(lambda: xb[rows, :], slots * PD, (r + 1) % 2, lambda c: None, None)
+        at = slice(QT + first, QT + first + slots * PD)
         hid[at, :] = h
         nrm[at, :] = n
         inv[at, :] = iv
-    for k in range(PD):
-        pall[k, 0:PLN, :] = nrm[pl.ds(QT + k, PLN, stride=PD), :].astype(bf16)
-
-    p_copy = remote(pall.at[pl.ds(0, PD)], pall.at[pl.ds(PD, PD)], p_sem.at[0], p_sem.at[1], (rep, other))
-    p_copy.start()
+        for k in range(PD):
+            pall[k, r * TS : r * TS + slots, :] = nrm[pl.ds(QT + first + k, slots, stride=PD), :].astype(bf16)
+        p_copy(r).start()
+        if r == 0:
+            stage0 = qall.at[0, pl.ds(0, 3)]
+            q_copy(stage0, 0, at_z(1)).wait_recv()
+            for d in (2, 1, 3):
+                q_copy(qall.at[:, x, low], 1, at_x(d)).start()
+                q_copy(qall.at[z, :, high], 1, at_z(d)).start()
+
+    p_all = remote(pall.at[pl.ds(0, PD)], pall.at[pl.ds(PD, PD)], p_sem.at[0], p_sem.at[1], (rep, other))
 
     def make_ptr(h):
         v = pall[h * PD : (h + 1) * PD].reshape(HALF, E).astype(f32)
@@ -218,8 +241,9 @@
 
     scale = math.log2(math.e) / temper
 
-    def forward(j, h):
-        q = qall[j]
+    def forward(row, i, h):
+        j = row * 4 + i
+        q = qall[row, i]
         for k in range(PD):
             p = h * PD + k
             s = lax.dot_general(pall[p], q, (((1,), (1,)), ((), ())), preferred_element_type=f32)
@@ -229,34 +253,23 @@
                 wts[j, p * PP : (p + 1) * PP, c * 128 : (c + 1) * 128] = w
                 tot[j, c, p : p + 1, :] = jnp.sum(w, axis=0, keepdims=True)
 
-    make_ptr(0)
-
-    @pl.loop(0, 4)
-    def _(g):
-        row = lax.rem(z + 4 - g, 4)
-        base = 4 * row
-
-        @pl.when(g == 0)
-        def _():
-            several(qall, 3, q_ss, q_rs.at[row]).wait_recv()
-
-        @pl.when(g > 0)
-        def _():
-            several(qall, 4, q_ss, q_rs.at[row]).wait_recv()
-
-        for i in range(4):
-            forward(base + i, 0)
-
     k_copy.wait_recv()
-    p_copy.wait_recv()
-    several(axall, ZX - 1, a_ss, a_rs).wait_recv()
     make_masks(kpr, PD)
-    make_ptr(1)
+
+    stage1 = qall.at[pl.ds(0, 3)]
+    q_copy(stage1, 1, at_z(1)).wait_recv()
 
     @pl.loop(0, 4)
     def _(g):
         for i in range(4):
-            forward(4 * g + i, 1)
+            forward(g, i, 0)
+
+    p_all.wait_recv()
+    several(axall, ZX - 1, a_ss, a_rs).wait_recv()
+    @pl.loop(0, 4)
+    def _(g):
+        for i in range(4):
+            forward(g, i, 1)
 
     shape4 = (ZX, 2, 8, 128)
     flat = (ZX * 2 * 8, 128)
@@ -281,6 +294,8 @@
     for k in far_first:
         m_copy(zx, member(k)).start()
 
+    make_ptr(0)
+    make_ptr(1)
     several(msg, ZX - 1, m_ss, m_rs).wait_recv()
 
     both = jnp.sum(msg[...], axis=0)
@@ -338,7 +353,7 @@
                         sgw[k * PP : (k + 1) * PP, i * QT + c * 128 : i * QT + (c + 1) * 128] = weighted(
                             4 * g + i, c, h * PD + k
                         )
-            q4 = qall[pl.ds(4 * g, 4)].reshape(4 * QT, E)
+            q4 = qall[g].reshape(4 * QT, E)
             part = jnp.dot(sgw[...], q4, preferred_element_type=f32)
 
             @pl.when(g == 0)
@@ -417,7 +432,8 @@
 
     gr_out[...] = grb[...].astype(f32)
 
-    several(qall, ZX - 1, q_ss, q_rs.at[0]).wait_send()
+    q_copy(stage0, 0, at_z(1)).wait_send()
+    q_copy(stage1, 1, at_z(1)).wait_send()
     several(axall, ZX - 1, a_ss, a_rs).wait_send()
     several(msg, ZX - 1, m_ss, m_rs).wait_send()
     several(qg, ZX - 1, g_ss, g_rs).wait_send()
@@ -426,7 +442,7 @@
     several(mid, YC - 1, c_ss, c_rs).wait_send()
     several(lmsg, YC - 1, l_ss, l_rs).wait_send()
     k_copy.wait_send()
-    p_copy.wait_send()
+    p_all.wait_send()
     pg_copy.wait_send()
 
 
@@ -475,7 +491,7 @@
             pltpu.VMEM((QT + PT, D), bf16),
             pltpu.VMEM((QT + PT, E), f32),
             pltpu.VMEM((QT + PT, E), f32),
-            pltpu.VMEM((ZX, QT, E), bf16),
+            pltpu.VMEM((4, 4, QT, E), bf16),
             pltpu.VMEM((2 * PD, PP, E), bf16),
             pltpu.VMEM((E, 2 * HALF), bf16),
             quad,
@@ -498,7 +514,7 @@
             pltpu.VMEM((YC, CH, E), bf16),
             pltpu.VMEM((D, E), bf16),
             dma((2,)), dma((2,)), dma((2,)),
-            dma, dma((4,)), dma, dma, dma((2,)), dma((2,)), dma, dma, dma, dma,
+            dma, dma((2,)), dma, dma, dma((2,)), dma((2,)), dma, dma, dma, dma,
             dma, dma, dma((2,)), dma, dma, dma, dma, dma, dma, dma((9,)),
         ],
         compiler_params=pltpu.CompilerParams(

time: 70.7 us -> 68.9 us (0.975)
  Pallas kernels: 69.8 us -> 67.9 us
    pallas_call x1, Pallas kernels: 67.8 us -> 65.8 us  [per_device(): pl.pallas_call(kernel, name='step', out_shape=tuple((pltpu.VMEM(o.shape,...]
where the time goes in v4:
time: 68.9 us; the launch traced here: 68.7 us
  Pallas kernels  67.9 us (99%)
  between operations  0.8 us (1%)
    pallas_call x1, Pallas kernels, per_device(): pl.pallas_call(kernel, name='step', out_shape=tuple((pltpu.VMEM(o.shape,...  65.8 us
    pallas_call x1, Pallas kernels, per_device(): pl.pallas_call(hand_out, name='hand_out', out_shape=outs, in_specs=[vm, v...  2.03 us

profile of v4, /device:TPU:0, one launch (start us, length us, event | category | flops | bytes accessed | tf_op | source)
XLA Modules:
  0.0 68.7 jit_solution(4351042211815801225)
XLA Ops:
  0.6 65.8 %step.1 = (f32[1,1]{1,0:T(1,128)}, f32[720,128]{1,0:T(8,128)S(1)}, f32[768,128]{1,0:T(8,128)S(1)}) custom-call(bf16[256,768]{1,0:T(8,128)(2,1)} %bitcast.8, bf16[180,4,768]{2,1,0:T(4,128)(2,1)} %bitcast.7, s32[8]{0:T(128)} %qlen_in.1, s32[4]{0:T(128)} %plen_in.1, s32[4,180]{1,0:T(4,128)} %ids_in.1, s32[8]{0:T(128)} %pos_in.1, bf16[768,3072]{1,0:T(8,128)(2,1)} %upw.1, ...), custom_call_target="tpu_custom_call" | custom-call | tf_op jit(solution)/shard_map/step/pallas_call | solution.py:468
  66.5 2.0 %hand_out.1 = (f32[1,1]{1,0:T(1,128)}, f32[720,128]{1,0:T(8,128)}, f32[768,128]{1,0:T(8,128)}) custom-call(f32[1,1]{1,0:T(1,128)} %get-tuple-element.9.loss, f32[720,128]{1,0:T(8,128)S(1)} %get-tuple-element.10.pgrad, f32[768,128]{1,0:T(8,128)S(1)} %get-tuple-element.11.grad), custom_call_target="tpu_custom_call" | custom-call | tf_op jit(solution)/shard_map/hand_out/pallas_call | solution.py:527

commit v5 on v4

--- a/solution.py
+++ b/solution.py
@@ -99,12 +99,9 @@
 
     barrier = pltpu.get_barrier_semaphore()
 
-    @pl.loop(1, ZX)
-    def _(k):
+    for k in range(1, ZX):
         pl.semaphore_signal(barrier, inc=1, device_id=row_dev(member(k)), device_id_type=MESH)
-
-    @pl.loop(1, YC)
-    def _(k):
+    for k in range(1, YC):
         pl.semaphore_signal(barrier, inc=1, device_id=col_dev(lax.rem(col + k, YC)), device_id_type=MESH)
 
     pall[0:PD] = jnp.zeros((PD, PP, E), bf16)
@@ -232,6 +229,8 @@
             for d in (2, 1, 3):
                 q_copy(qall.at[:, x, low], 1, at_x(d)).start()
                 q_copy(qall.at[z, :, high], 1, at_z(d)).start()
+            k_copy.wait_recv()
+            make_masks(kpr, PD)
 
     p_all = remote(pall.at[pl.ds(0, PD)], pall.at[pl.ds(PD, PD)], p_sem.at[0], p_sem.at[1], (rep, other))
 
@@ -253,8 +252,6 @@
                 wts[j, p * PP : (p + 1) * PP, c * 128 : (c + 1) * 128] = w
                 tot[j, c, p : p + 1, :] = jnp.sum(w, axis=0, keepdims=True)
 
-    k_copy.wait_recv()
-    make_masks(kpr, PD)
 
     stage1 = qall.at[pl.ds(0, 3)]
     q_copy(stage1, 1, at_z(1)).wait_recv()

time: 68.9 us -> 68.6 us (level)
  no operation moved by 1% of the time
where the time goes in v5:
time: 68.6 us; the launch traced here: 68.5 us
  Pallas kernels  67.7 us (99%)
  between operations  0.8 us (1%)
    pallas_call x1, Pallas kernels, per_device(): pl.pallas_call(kernel, name='step', out_shape=tuple((pltpu.VMEM(o.shape,...  65.7 us
    pallas_call x1, Pallas kernels, per_device(): pl.pallas_call(hand_out, name='hand_out', out_shape=outs, in_specs=[vm, v...  2.03 us

profile of v5, /device:TPU:0, one launch (start us, length us, event | category | flops | bytes accessed | tf_op | source)
XLA Modules:
  0.0 68.5 jit_solution(2144083113683750526)
XLA Ops:
  0.6 65.7 %step.1 = (f32[1,1]{1,0:T(1,128)}, f32[720,128]{1,0:T(8,128)S(1)}, f32[768,128]{1,0:T(8,128)S(1)}) custom-call(bf16[256,768]{1,0:T(8,128)(2,1)} %bitcast.8, bf16[180,4,768]{2,1,0:T(4,128)(2,1)} %bitcast.7, s32[8]{0:T(128)} %qlen_in.1, s32[4]{0:T(128)} %plen_in.1, s32[4,180]{1,0:T(4,128)} %ids_in.1, s32[8]{0:T(128)} %pos_in.1, bf16[768,3072]{1,0:T(8,128)(2,1)} %upw.1, ...), custom_call_target="tpu_custom_call" | custom-call | tf_op jit(solution)/shard_map/step/pallas_call | solution.py:465
  66.3 2.0 %hand_out.1 = (f32[1,1]{1,0:T(1,128)}, f32[720,128]{1,0:T(8,128)}, f32[768,128]{1,0:T(8,128)}) custom-call(f32[1,1]{1,0:T(1,128)} %get-tuple-element.9.loss, f32[720,128]{1,0:T(8,128)S(1)} %get-tuple-element.10.pgrad, f32[768,128]{1,0:T(8,128)S(1)} %get-tuple-element.11.grad), custom_call_target="tpu_custom_call" | custom-call | tf_op jit(solution)/shard_map/hand_out/pallas_call | solution.py:524
